TPU v7x, 32 devices: a whole 2x2x4 slice. The times are simulated.
32 devices in a mesh: mode: 8 (over y, x, core), tm: 4 (over z).
Axes of the slice: x: 2, y: 2, z: 4, core: 2. Of those that a mesh axis runs over, the one named last changes fastest.
Arguments:
- field: float32 [2, 128, 65536], P(None, 'mode', 'tm'), may hold values from -1.8 to 1.8
- beta: float32 [3, 128], P(None, 'mode'), may hold values from -1 to 1
- quartets: int32 [4, 1024], replicated, may hold values from 0 to 127
- intersections: float32 [1024], replicated, may hold values from -0.12 to 0.12
Outputs:
- field_out: float32 [2, 128, 65536], P(None, 'mode', 'tm')
- errors: float32 [2, 128], P(None, 'mode')
All inputs are finite; a program needn't handle non-finite values.
Results may differ from a plain program's by a relative error of at most 0.0003.
Values sent between devices are 32-bit elements; how exact they have to be, the bound alone decides.
A program may use at most 128 MiB of HBM per device.

v0:
```python
import functools
import math

import jax
import jax.numpy as jnp
from jax import lax
from jax.experimental import pallas as pl
from jax.experimental.pallas import tpu as pltpu
from jax.sharding import PartitionSpec as P

RADIX = 256
STEPS = 2


epsilon = 1e-06


def phase_of(offset, slope, curve, frequency):
    return math.pi * offset + 300.0 * slope * frequency + 3000.0 * curve * frequency * frequency


def triple_product(left_field, middle_field, conj_field):
    prod_re = left_field[0] * middle_field[0] - left_field[1] * middle_field[1]
    prod_im = left_field[0] * middle_field[1] + left_field[1] * middle_field[0]
    out_re = prod_re * conj_field[0] + prod_im * conj_field[1]
    out_im = prod_im * conj_field[0] - prod_re * conj_field[1]
    return (out_re, out_im)


def contract(form, first_operand, second_operand):
    return jnp.einsum(form, first_operand, second_operand, precision=lax.Precision.HIGHEST)


def rotate(real_part, imag_part, angle):
    cosine = jnp.cos(angle)
    sine_part = jnp.sin(angle)
    return (real_part * cosine - imag_part * sine_part, real_part * sine_part + imag_part * cosine)


def dft_tables(length):
    positions = lax.iota(jnp.int32, length)
    product = positions[:, None] * positions[None, :] % length
    angle = -2.0 * math.pi / length * product.astype(jnp.float32)
    return (jnp.cos(angle), jnp.sin(angle))


def to_columns(state):
    return lax.all_to_all(state, "tm", split_axis=3, concat_axis=2, tiled=True)


def to_rows(state):
    return lax.all_to_all(state, "tm", split_axis=2, concat_axis=3, tiled=True)


def linear_step(state, beta, table_re, table_im):
    radix_size = table_re.shape[0]
    total_time = radix_size * radix_size
    cols_local = state.shape[3]
    tm_index = lax.axis_index("tm")
    head_re = contract("ka,mab->mkb", table_re, state[0]) - contract(
        "ka,mab->mkb", table_im, state[1]
    )
    head_im = contract("ka,mab->mkb", table_re, state[1]) + contract(
        "ka,mab->mkb", table_im, state[0]
    )
    column = tm_index * cols_local + lax.iota(jnp.int32, cols_local)
    row_position = lax.iota(jnp.int32, radix_size)
    twist = (
        -2.0
        * math.pi
        / total_time
        * (row_position[:, None] * column[None, :] % total_time).astype(jnp.float32)
    )
    head_re, head_im = rotate(head_re, head_im, twist[None])
    turned = lax.all_to_all(
        jnp.stack([head_re, head_im]), "tm", split_axis=2, concat_axis=3, tiled=True
    )
    spec_re = contract("mcb,kb->mck", turned[0], table_re) - contract(
        "mcb,kb->mck", turned[1], table_im
    )
    spec_im = contract("mcb,kb->mck", turned[1], table_re) + contract(
        "mcb,kb->mck", turned[0], table_im
    )
    rows_local = turned.shape[2]
    first_index = tm_index * rows_local + lax.iota(jnp.int32, rows_local)
    wave = first_index[:, None] + radix_size * row_position[None, :]
    signed = jnp.where(wave < total_time // 2, wave, wave - total_time)
    frequency = signed.astype(jnp.float32) / (total_time / 2)
    angle = phase_of(
        beta[0][:, None, None], beta[1][:, None, None], beta[2][:, None, None], frequency[None]
    )
    spec_re, spec_im = rotate(spec_re, spec_im, angle)
    back_re = contract("mck,kb->mcb", spec_re, table_re) + contract(
        "mck,kb->mcb", spec_im, table_im
    )
    back_im = contract("mck,kb->mcb", spec_im, table_re) - contract(
        "mck,kb->mcb", spec_re, table_im
    )
    untwist = (
        2.0
        * math.pi
        / total_time
        * (first_index[:, None] * row_position[None, :] % total_time).astype(jnp.float32)
    )
    back_re, back_im = rotate(back_re, back_im, untwist[None])
    gathered = lax.all_to_all(
        jnp.stack([back_re, back_im]), "tm", split_axis=3, concat_axis=2, tiled=True
    )
    scale = 1.0 / total_time
    out_re = (
        contract("ka,mkb->mab", table_re, gathered[0])
        + contract("ka,mkb->mab", table_im, gathered[1])
    ) * scale
    out_im = (
        contract("ka,mkb->mab", table_re, gathered[1])
        - contract("ka,mkb->mab", table_im, gathered[0])
    ) * scale
    return jnp.stack([out_re, out_im])


def kerr_term(fields, quartets, intersections):
    count = quartets.shape[1]
    block_size = min(512, count)
    blocks = count // block_size
    grouped = quartets.reshape(4, blocks, block_size).transpose(1, 0, 2)
    weights = intersections.reshape(blocks, block_size)
    modes_all = fields.shape[1]
    mode_ids = lax.iota(jnp.int32, modes_all)

    def accumulate(running, block_item):
        indices, weight = block_item
        out_re, out_im = triple_product(
            jnp.take(fields, indices[1], axis=1),
            jnp.take(fields, indices[2], axis=1),
            jnp.take(fields, indices[3], axis=1),
        )
        owner = (indices[0][None, :] == mode_ids[:, None]).astype(jnp.float32) * weight[None, :]
        add_re = contract("pq,qt->pt", owner, -out_im)
        add_im = contract("pq,qt->pt", owner, out_re)
        return (running + jnp.stack([add_re, add_im]), None)

    running, unused = lax.scan(accumulate, jnp.zeros_like(fields), (grouped, weights))
    return running


def kerr_step(flat, quartets, intersections):
    spread = lax.all_to_all(flat, "mode", split_axis=2, concat_axis=1, tiled=True)
    first = kerr_term(spread, quartets, intersections)
    second = kerr_term(spread + first, quartets, intersections)
    updated = spread + 0.5 * (first + second)
    estimate = 0.5 * (second - first)
    returned, estimate_home = (
        lax.all_to_all(updated, "mode", split_axis=1, concat_axis=2, tiled=True),
        lax.all_to_all(estimate, "mode", split_axis=1, concat_axis=2, tiled=True),
    )
    error_part = jnp.sum(estimate_home * estimate_home, axis=(0, 2))
    field_part = jnp.sum(returned * returned, axis=(0, 2))
    return (returned, error_part, field_part)


def shards_general(field, beta, quartets, intersections):
    modes_local = field.shape[1]
    time_local = field.shape[2]
    table_re, table_im = dft_tables(RADIX)
    state = field.reshape(2, modes_local, time_local // RADIX, RADIX)
    state = to_columns(state)
    error_rows = []
    for step_index in range(STEPS):
        columns = state
        columns = linear_step(columns, beta, table_re, table_im)
        updated, error_part, field_part = kerr_step(
            columns.reshape(2, modes_local, time_local), quartets, intersections
        )
        error_sq, field_sq = lax.psum((error_part, field_part), "tm")
        error_rows.append(jnp.sqrt(error_sq / (field_sq + epsilon)))
        state = updated.reshape(columns.shape)
    state = to_rows(state)
    errors = jnp.stack(error_rows)
    return (state.reshape(2, modes_local, time_local), errors)


UNROLL = 8
CHAINS = 1


def split(value):
    high = value.astype(jnp.bfloat16)
    low = (value - high.astype(jnp.float32)).astype(jnp.bfloat16)
    return high, low


def split_table(value):
    high = lax.reduce_precision(value, exponent_bits=8, mantissa_bits=7)
    return high.astype(jnp.bfloat16), (value - high).astype(jnp.bfloat16)


def product(left, right):
    dot = lambda a, b: jnp.dot(a, b, preferred_element_type=jnp.float32)
    return dot(left[0], right[0]) + (dot(left[0], right[1]) + dot(left[1], right[0]))


def spectral_kernel(x_ref, m1h, m1l, m2h, m2l, twist_ref, rotor_ref, out_ref):
    radix = twist_ref.shape[1]
    m1 = (m1h[...], m1l[...])
    m2 = (m2h[...], m2l[...])
    real = x_ref[:, 0, 0].reshape(radix, radix)
    imag = x_ref[:, 1, 0].reshape(radix, radix)
    head = product(m1, split(jnp.concatenate([real, imag], axis=0)))
    head_re, head_im = head[:radix], head[radix:]
    tw_re, tw_im = twist_ref[0], twist_ref[1]
    re = head_re * tw_re - head_im * tw_im
    im = head_re * tw_im + head_im * tw_re
    spec = product(split(jnp.concatenate([re, im], axis=1)), m2)
    spec_re, spec_im = spec[:, :radix], spec[:, radix:]
    ro_re, ro_im = rotor_ref[0, 0], rotor_ref[1, 0]
    re = spec_re * ro_re - spec_im * ro_im
    im = spec_re * ro_im + spec_im * ro_re
    back = product(split(jnp.concatenate([re, im], axis=1)), m1)
    back_re, back_im = back[:, :radix], back[:, radix:]
    re = back_re * tw_re + back_im * tw_im
    im = back_im * tw_re - back_re * tw_im
    out = product(m2, split(jnp.concatenate([re, im], axis=0)))
    shape = out_ref.shape[:1] + out_ref.shape[3:]
    out_ref[:, 0, 0] = out[:radix].reshape(shape)
    out_ref[:, 1, 0] = out[radix:].reshape(shape)


def spectral(x, tables, twist, rotor, blocks):
    count, _, modes, rows, radix = x.shape
    whole = lambda a: pl.BlockSpec(a.shape, lambda g: (0,) * a.ndim)
    return pl.pallas_call(
        spectral_kernel,
        grid=(modes,),
        in_specs=[pl.BlockSpec((count, 2, 1, rows, radix), lambda g: (0, 0, g, 0, 0))]
        + [whole(t) for t in tables]
        + [whole(twist), pl.BlockSpec((2, 1, radix, radix), lambda g: (0, g, 0, 0))],
        out_specs=pl.BlockSpec((blocks, 2, 1, radix // blocks, radix), lambda g: (0, 0, g, 0, 0)),
        out_shape=jax.ShapeDtypeStruct((blocks, 2, modes, radix // blocks, radix), jnp.float32),
        compiler_params=pltpu.CompilerParams(vmem_limit_bytes=48 * 1024 * 1024),
        name="spectral",
    )(x, *tables, twist, rotor)


def kerr_kernel(stride, quartets, weights, lin_ref, out_ref, err_ref, mid_ref, *accs):
    chains = len(accs) // 2
    count = weights.shape[0]
    unroll = UNROLL if count % UNROLL == 0 else 1

    def evaluate(src, totals):
        for total in totals:
            total[...] = jnp.zeros_like(total)

        def chunk(c, carry):
            pending = []
            for u in range(unroll):
                q = c * unroll + u
                l, m, n = quartets[4 * q + 1], quartets[4 * q + 2], quartets[4 * q + 3]
                w = weights[q]
                re, im = triple_product(
                    (src[l], src[l + stride]), (src[m], src[m + stride]), (src[n], src[n + stride])
                )
                pending.append((quartets[4 * q], -w * im, w * re))
            for u, (p, re, im) in enumerate(pending):
                total = totals[u % chains]
                total[p] += re
                total[p + stride] += im
            return carry

        lax.fori_loop(0, count // unroll, chunk, 0)

    evaluate(lin_ref, accs[:chains])
    first_ref = accs[0]

    def combine(i, carry):
        first_ref[i] = sum(total[i] for total in accs[:chains])
        mid_ref[i] = lin_ref[i] + first_ref[i]
        return carry

    lax.fori_loop(0, lin_ref.shape[0], combine, 0, unroll=4)
    evaluate(mid_ref, accs[chains:])

    def finish(i, carry):
        first, second = first_ref[i], sum(total[i] for total in accs[chains:])
        new = lin_ref[i] + 0.5 * (first + second)
        estimate = 0.5 * (second - first)
        out_ref[i] = new
        err_ref[0, pl.ds(i, 1)] = jnp.sum(estimate * estimate, axis=0, keepdims=True)
        err_ref[1, pl.ds(i, 1)] = jnp.sum(new * new, axis=0, keepdims=True)
        return carry

    lax.fori_loop(0, lin_ref.shape[0], finish, 0, unroll=4)


def kerr(lin, quartets, weights, stride):
    planes, rows, lanes = lin.shape
    vmem = pl.BlockSpec(memory_space=pltpu.VMEM)
    smem = pl.BlockSpec(memory_space=pltpu.SMEM)
    return pl.pallas_call(
        functools.partial(kerr_kernel, stride),
        in_specs=[smem, smem, vmem],
        out_specs=[vmem, vmem],
        out_shape=[
            jax.ShapeDtypeStruct(lin.shape, jnp.float32),
            jax.ShapeDtypeStruct((2, planes, lanes), jnp.float32),
        ],
        scratch_shapes=[pltpu.VMEM(lin.shape, jnp.float32)] * (1 + 2 * CHAINS),
        compiler_params=pltpu.CompilerParams(vmem_limit_bytes=40 * 1024 * 1024),
        name="kerr",
    )(quartets, weights, lin)


def shards(ways, field, beta, quartets, intersections):
    mode_ways, tm_ways = ways
    devices = mode_ways * tm_ways
    _, modes_local, time_local = field.shape
    total_time = time_local * tm_ways
    radix = math.isqrt(total_time)
    own = modes_local // tm_ways
    modes_all = modes_local * mode_ways
    rows = radix // devices
    tm_index = lax.axis_index("tm")

    table_re, table_im = dft_tables(radix)
    m1 = jnp.concatenate(
        [jnp.concatenate([table_re, -table_im], 1), jnp.concatenate([table_im, table_re], 1)], 0
    )
    m2 = jnp.concatenate(
        [jnp.concatenate([table_re, table_im], 1), jnp.concatenate([-table_im, table_re], 1)], 0
    )
    tables = split_table(m1) + split_table(m2)
    position = lax.iota(jnp.int32, radix)
    angle = (
        -2.0
        * math.pi
        / total_time
        * (position[:, None] * position[None, :] % total_time).astype(jnp.float32)
    )
    twist = jnp.stack([jnp.cos(angle), jnp.sin(angle)])
    wave = position[:, None] + radix * position[None, :]
    signed = jnp.where(wave < total_time // 2, wave, wave - total_time)
    frequency = signed.astype(jnp.float32) / (total_time / 2)
    mine = lax.dynamic_slice_in_dim(beta, tm_index * own, own, axis=1)
    phase = phase_of(
        mine[0][:, None, None], mine[1][:, None, None], mine[2][:, None, None], frequency[None]
    )
    rotor = jnp.stack([jnp.cos(phase), jnp.sin(phase)]) * (1.0 / total_time)

    holder = quartets % modes_local // own * mode_ways + quartets // modes_local
    planes = (holder * (2 * own) + quartets % own).T.reshape(-1)

    state = field.reshape(2, tm_ways, own, time_local // radix, radix).transpose(1, 0, 2, 3, 4)
    state = lax.all_to_all(state, "tm", split_axis=0, concat_axis=0, tiled=True)
    sums = []
    for step_index in range(STEPS):
        state = spectral(state, tables, twist, rotor, devices)
        state = lax.all_to_all(state, ("tm", "mode"), split_axis=0, concat_axis=0, tiled=True)
        flat, part = kerr(
            state.reshape(2 * modes_all, rows, radix), planes, intersections, own
        )
        sums.append(part)
        state = flat.reshape(devices, 2, own, rows, radix)
        if step_index < STEPS - 1:
            state = lax.all_to_all(state, ("tm", "mode"), split_axis=0, concat_axis=0, tiled=True)
    state = state.reshape(tm_ways, mode_ways, 2, own, rows, radix)
    state = lax.all_to_all(state, "mode", split_axis=1, concat_axis=1, tiled=True)
    out = state.transpose(2, 0, 3, 1, 4, 5).reshape(2, modes_local, time_local)

    norms = jnp.sum(jnp.stack(sums), axis=-1).reshape(STEPS, 2, tm_ways, mode_ways, 2, own)
    norms = jnp.sum(norms, axis=4).transpose(3, 0, 1, 2, 4).reshape(mode_ways, -1)
    norms = jnp.broadcast_to(norms[:, None], (mode_ways, tm_ways, norms.shape[1]))
    norms = norms.reshape(devices, 1, -1)
    norms = lax.all_to_all(norms, ("mode", "tm"), split_axis=0, concat_axis=0, tiled=True)
    norms = jnp.sum(norms, axis=0).reshape(STEPS, 2, modes_local)
    errors = jnp.sqrt(norms[:, 0] / (norms[:, 1] + epsilon))
    return (out, errors)


def solution(mesh):
    placed = (P(None, "mode", "tm"), P(None, "mode"), P(), P())

    def body(field, beta, quartets, intersections):
        mode_ways, tm_ways = mesh.shape["mode"], mesh.shape["tm"]
        devices = mode_ways * tm_ways
        if field.shape[1] % tm_ways == 0 and RADIX % (8 * devices) == 0:
            return shards((mode_ways, tm_ways), field, beta, quartets, intersections)
        return shards_general(field, beta, quartets, intersections)

    return jax.shard_map(
        body,
        mesh=mesh,
        in_specs=placed,
        out_specs=(P(None, "mode", "tm"), P(None, "mode")),
        check_vma=False,
    )
```

profile of v0, /device:TPU:0, one launch (start us, length us, event | category | flops | bytes accessed | tf_op | source)
XLA Modules:
  0.0 326.8 jit_solution(505043676764083640)
XLA Ops:
  0.6 0.0 copy-start
  0.6 2.2 copy.22
  2.9 1.5 copy.24
  4.3 6.3 %all-to-all-start = ((f32[4,2,4,64,256]{4,3,2,1,0:T(8,128)}), f32[4,2,4,64,256]{4,3,2,1,0:T(8,128)}, u32[]{:S(2)}, u32[]{:S(2)}) async-start(f32[4,2,4,64,256]{4,3,2,1,0:T(8,128)} %bitcast.27), calls=%async_computation | async-start | bytes 4194304 | tf_op jit(solution)/shard_map/all_to_all | solution.py:352
  10.7 0.0 copy-done
  10.7 0.1 constant_dynamic-slice_fusion
  10.8 1.0 fusion.24
  11.8 1.0 fusion.22
  12.8 1.0 fusion.20
  13.9 0.1 fusion.13
  14.0 3.8 %fusion.5 = (f32[1,4,256,256]{3,2,1,0:T(8,128)S(1)}, f32[1,4,256,256]{3,2,1,0:T(8,128)S(1)}) fusion(f32[4]{0:T(128)S(1)} %get-tuple-element.17, f32[256,256]{1,0:T(8,128)S(1)} %fusion.13, f32[4]{0:T(128)S(1)} %get-tuple-element.18, f32[4]{0:T(128)S(1)} %get-tuple-element.16), kind=kLoop, calls=%fused_computation.17 | loop fusion | flops 1310720 | bytes 2359344 | tf_op jit(solution)/shard_map/cos | solution.py:346
  17.8 1.5 maximum_multiply_fusion.rotor_ref
  19.3 0.3 fusion.3
  19.6 0.0 copy-start.1
  19.6 0.0 copy-start.3
  19.6 0.0 copy-start.5
  19.6 39.4 %all-to-all-done.x_ref = f32[4,2,4,64,256]{4,3,2,1,0:T(8,128)} async-done(((f32[4,2,4,64,256]{4,3,2,1,0:T(8,128)}), f32[4,2,4,64,256]{4,3,2,1,0:T(8,128)}, u32[]{:S(2)}, u32[]{:S(2)}) %all-to-all-start) | async-done | bytes 2097184 | tf_op jit(solution)/shard_map/all_to_all | solution.py:352
  59.0 13.9 %spectral.2 = f32[32,2,4,8,256]{4,3,2,1,0:T(8,128)} custom-call(f32[4,2,4,64,256]{4,3,2,1,0:T(8,128)} %all-to-all-done.x_ref, bf16[512,512]{1,0:T(8,128)(2,1)S(1)} %get-tuple-element.12.m1h, bf16[512,512]{1,0:T(8,128)(2,1)S(1)} %get-tuple-element.11.m1l, bf16[512,512]{1,0:T(8,128)(2,1)S(1)} %get-tuple-element.13.m2h, ...), custom_call_target="tpu_custom_call" | custom-call | tf_op jit(solution)/shard_map/spectral/pallas_call | solution.py:231
  72.9 0.0 copy-done.1
  72.9 0.0 copy-done.3
  72.9 0.0 copy-done.5
  72.9 0.0 copy-start.8
  72.9 0.0 copy-start.7
  72.9 3.7 %all-to-all-start.1 = ((f32[32,2,4,8,256]{4,3,2,1,0:T(8,128)}), f32[32,2,4,8,256]{4,3,2,1,0:T(8,128)S(1)}, u32[]{:S(2)}, u32[]{:S(2)}) async-start(f32[32,2,4,8,256]{4,3,2,1,0:T(8,128)} %spectral.2), calls=%async_computation.1 | async-start | bytes 4194304 | tf_op jit(solution)/shard_map/all_to_all | solution.py:356
  76.6 0.0 copy-done.8
  76.6 0.1 fusion.30
  76.7 1.0 copy.16
  77.7 1.3 reshape.184.quartets
  79.0 46.3 %all-to-all-done.1 = f32[32,2,4,8,256]{4,3,2,1,0:T(8,128)S(1)} async-done(((f32[32,2,4,8,256]{4,3,2,1,0:T(8,128)}), f32[32,2,4,8,256]{4,3,2,1,0:T(8,128)S(1)}, u32[]{:S(2)}, u32[]{:S(2)}) %all-to-all-start.1) | async-done | bytes 2097184 | tf_op jit(solution)/shard_map/all_to_all | solution.py:356
  125.3 0.0 copy-done.7
  125.4 18.4 %kerr.2 = (f32[256,8,256]{2,1,0:T(8,128)S(1)}, f32[2,256,256]{2,1,0:T(8,128)S(1)}) custom-call(s32[4096]{0:T(1024)S(1)} %reshape.184.quartets, f32[1024]{0:T(1024)S(1)} %copy-done.7, f32[256,8,256]{2,1,0:T(8,128)S(1)} %bitcast.28), custom_call_target="tpu_custom_call" | custom-call | tf_op jit(solution)/shard_map/kerr/pallas_call | solution.py:298
  143.7 0.0 copy-start.2
  143.7 0.0 copy-start.4
  143.8 0.0 copy-start.6
  143.8 52.7 %all_to_all.30.x_ref = f32[32,2,4,8,256]{4,3,2,1,0:T(8,128)} all-to-all(f32[32,2,4,8,256]{4,3,2,1,0:T(8,128)S(1)} %bitcast.31), channel_id=1, replica_groups=mesh['mode'=8,'tm'=4] {'tm','mode'}, dimensions={0} | all-to-all | bytes 4194304 | tf_op jit(solution)/shard_map/all_to_all | solution.py:363
  196.4 0.0 copy-done.2
  196.4 0.0 copy-done.4
  196.5 0.0 copy-done.6
  196.5 13.0 %spectral.3 = f32[32,2,4,8,256]{4,3,2,1,0:T(8,128)S(1)} custom-call(f32[32,2,4,8,256]{4,3,2,1,0:T(8,128)} %all_to_all.30.x_ref, bf16[512,512]{1,0:T(8,128)(2,1)S(1)} %copy-done.4, bf16[512,512]{1,0:T(8,128)(2,1)S(1)} %copy-done.2, bf16[512,512]{1,0:T(8,128)(2,1)S(1)} %copy-done.6, bf16[512,512]{1,0:T(8,128)(2,1)S(1)} %get-tuple-element.10.m2l, ...), custom_call_target="tpu_custom_call" | custom-call | tf_op jit(solution)/shard_map/spectral/pallas_call | solution.py:231
  209.5 52.2 %all_to_all.31 = f32[32,2,4,8,256]{4,3,2,1,0:T(8,128)S(1)} all-to-all(f32[32,2,4,8,256]{4,3,2,1,0:T(8,128)S(1)} %spectral.3), channel_id=1, replica_groups=mesh['mode'=8,'tm'=4] {'tm','mode'}, dimensions={0} | all-to-all | bytes 4194304 | tf_op jit(solution)/shard_map/all_to_all | solution.py:356
  261.6 18.4 %kerr.3 = (f32[256,8,256]{2,1,0:T(8,128)S(1)}, f32[2,256,256]{2,1,0:T(8,128)S(1)}) custom-call(s32[4096]{0:T(1024)S(1)} %reshape.184.quartets, f32[1024]{0:T(1024)S(1)} %copy-done.7, f32[256,8,256]{2,1,0:T(8,128)S(1)} %bitcast.29), custom_call_target="tpu_custom_call" | custom-call | tf_op jit(solution)/shard_map/kerr/pallas_call | solution.py:298
  280.0 0.2 maximum_reduce_fusion
  280.2 0.2 reshape.190
  280.5 0.2 reduce_sum.28
  280.6 0.2 copy.20
  280.8 0.1 copy.21
  280.9 0.6 broadcast_in_dim.5
  281.5 3.7 %all-to-all-start.5 = ((f32[32,1,64]{2,1,0:T(1,128)}), f32[32,1,64]{2,1,0:T(1,128)S(1)}, u32[]{:S(2)}, u32[]{:S(2)}) async-start(f32[32,1,64]{2,1,0:T(1,128)} %bitcast.14), calls=%async_computation.5 | async-start | bytes 32768 | tf_op jit(solution)/shard_map/all_to_all | solution.py:372
  285.2 1.5 copy.18
  286.6 5.7 %all-to-all-done.5 = f32[32,1,64]{2,1,0:T(1,128)S(1)} async-done(((f32[32,1,64]{2,1,0:T(1,128)}), f32[32,1,64]{2,1,0:T(1,128)S(1)}, u32[]{:S(2)}, u32[]{:S(2)}) %all-to-all-start.5) | async-done | bytes 8224 | tf_op jit(solution)/shard_map/all_to_all | solution.py:372
  292.4 3.6 %all-to-all-start.4 = ((f32[4,8,2,4,8,256]{5,4,3,2,0,1:T(8,128)}), f32[4,8,2,4,8,256]{5,4,3,2,0,1:T(8,128)S(1)}, u32[]{:S(2)}, u32[]{:S(2)}) async-start(f32[4,8,2,4,8,256]{5,4,3,2,0,1:T(8,128)} %copy.18), calls=%async_computation.4 | async-start | bytes 4194304 | tf_op jit(solution)/shard_map/all_to_all | solution.py:365
  296.0 0.1 reduce_sum.29
  296.0 0.1 reshape.192
  296.1 0.6 fusion.35
  296.7 25.8 %all-to-all-done.4 = f32[4,8,2,4,8,256]{5,4,3,2,0,1:T(8,128)S(1)} async-done(((f32[4,8,2,4,8,256]{5,4,3,2,0,1:T(8,128)}), f32[4,8,2,4,8,256]{5,4,3,2,0,1:T(8,128)S(1)}, u32[]{:S(2)}, u32[]{:S(2)}) %all-to-all-start.4) | async-done | bytes 2097184 | tf_op jit(solution)/shard_map/all_to_all | solution.py:365
  322.5 1.6 copy.19
  324.1 2.7 reshape.189
  (3 shorter events, 0.0 us)
Async XLA Ops:
  0.6 10.1 %copy-start = (f32[3,16]{1,0:T(4,128)S(1)}, f32[3,16]{1,0:T(4,128)}, u32[]{:S(2)}) copy-start(f32[3,16]{1,0:T(4,128)} %param.5) | copy-start | bytes 580
  4.3 54.6 %all-to-all-start = ((f32[4,2,4,64,256]{4,3,2,1,0:T(8,128)}), f32[4,2,4,64,256]{4,3,2,1,0:T(8,128)}, u32[]{:S(2)}, u32[]{:S(2)}) async-start(f32[4,2,4,64,256]{4,3,2,1,0:T(8,128)} %bitcast.27), calls=%async_computation | async-start | bytes 4194304 | tf_op jit(solution)/shard_map/all_to_all | solution.py:352
  19.6 53.3 %copy-start.1 = (bf16[512,512]{1,0:T(8,128)(2,1)}, bf16[512,512]{1,0:T(8,128)(2,1)S(1)}, u32[]{:S(2)}) copy-start(bf16[512,512]{1,0:T(8,128)(2,1)S(1)} %get-tuple-element.11.m1l) | copy-start | bytes 1572868
  19.6 53.3 %copy-start.3 = (bf16[512,512]{1,0:T(8,128)(2,1)}, bf16[512,512]{1,0:T(8,128)(2,1)S(1)}, u32[]{:S(2)}) copy-start(bf16[512,512]{1,0:T(8,128)(2,1)S(1)} %get-tuple-element.12.m1h) | copy-start | bytes 1572868
  19.6 53.3 %copy-start.5 = (bf16[512,512]{1,0:T(8,128)(2,1)}, bf16[512,512]{1,0:T(8,128)(2,1)S(1)}, u32[]{:S(2)}) copy-start(bf16[512,512]{1,0:T(8,128)(2,1)S(1)} %get-tuple-element.13.m2h) | copy-start | bytes 1572868
  72.9 3.7 %copy-start.8 = (s32[4,1024]{1,0:T(4,128)S(1)}, s32[4,1024]{1,0:T(4,128)}, u32[]{:S(2)}) copy-start(s32[4,1024]{1,0:T(4,128)} %param.6) | copy-start | bytes 49156
  72.9 52.5 %copy-start.7 = (f32[1024]{0:T(1024)S(1)}, f32[1024]{0:T(1024)}, u32[]{:S(2)}) copy-start(f32[1024]{0:T(1024)} %weights.3) | copy-start | bytes 12292
  72.9 52.5 %all-to-all-start.1 = ((f32[32,2,4,8,256]{4,3,2,1,0:T(8,128)}), f32[32,2,4,8,256]{4,3,2,1,0:T(8,128)S(1)}, u32[]{:S(2)}, u32[]{:S(2)}) async-start(f32[32,2,4,8,256]{4,3,2,1,0:T(8,128)} %spectral.2), calls=%async_computation.1 | async-start | bytes 4194304 | tf_op jit(solution)/shard_map/all_to_all | solution.py:356
  143.7 52.7 %copy-start.2 = (bf16[512,512]{1,0:T(8,128)(2,1)S(1)}, bf16[512,512]{1,0:T(8,128)(2,1)}, u32[]{:S(2)}) copy-start(bf16[512,512]{1,0:T(8,128)(2,1)} %copy-done.1) | copy-start | bytes 1572868
  143.7 52.7 %copy-start.4 = (bf16[512,512]{1,0:T(8,128)(2,1)S(1)}, bf16[512,512]{1,0:T(8,128)(2,1)}, u32[]{:S(2)}) copy-start(bf16[512,512]{1,0:T(8,128)(2,1)} %copy-done.3) | copy-start | bytes 1572868
  143.8 52.7 %copy-start.6 = (bf16[512,512]{1,0:T(8,128)(2,1)S(1)}, bf16[512,512]{1,0:T(8,128)(2,1)}, u32[]{:S(2)}) copy-start(bf16[512,512]{1,0:T(8,128)(2,1)} %copy-done.5) | copy-start | bytes 1572868
  281.5 10.9 %all-to-all-start.5 = ((f32[32,1,64]{2,1,0:T(1,128)}), f32[32,1,64]{2,1,0:T(1,128)S(1)}, u32[]{:S(2)}, u32[]{:S(2)}) async-start(f32[32,1,64]{2,1,0:T(1,128)} %bitcast.14), calls=%async_computation.5 | async-start | bytes 32768 | tf_op jit(solution)/shard_map/all_to_all | solution.py:372
  292.4 30.2 %all-to-all-start.4 = ((f32[4,8,2,4,8,256]{5,4,3,2,0,1:T(8,128)}), f32[4,8,2,4,8,256]{5,4,3,2,0,1:T(8,128)S(1)}, u32[]{:S(2)}, u32[]{:S(2)}) async-start(f32[4,8,2,4,8,256]{5,4,3,2,0,1:T(8,128)} %copy.18), calls=%async_computation.4 | async-start | bytes 4194304 | tf_op jit(solution)/shard_map/all_to_all | solution.py:365
where the time goes:
time: 327 us
  waiting for transfers between devices  117 us (36%)
  blocking collectives  105 us (32%)
  Pallas kernels  63.6 us (19%)
  starting transfers between devices  17.3 us (5%)
  local copies, waits for them, and re-layouts  13.1 us (4%)
  other arithmetic  9.83 us (3%)
    all_to_all x2, blocking collectives, shards(): lax.all_to_all(state, ('tm', 'mode'), split_axis=0, concat_axis=0, tiled=...  105 us
    all_to_all x1, waiting for transfers between devices, shards(): lax.all_to_all(state, ('tm', 'mode'), split_axis=0, concat_axis=0, tiled=...  46.3 us
    all_to_all x1, waiting for transfers between devices, shards(): state = lax.all_to_all(state, 'tm', split_axis=0, concat_axis=0, tiled=True)  39.4 us
    pallas_call x2, Pallas kernels, kerr(): pl.pallas_call(functools.partial(kerr_kernel, stride), in_specs=[smem, sm...  36.8 us
    pallas_call x2, Pallas kernels, spectral(): pl.pallas_call(spectral_kernel, grid=(modes,), in_specs=[pl.BlockSpec((co...  26.9 us
    all_to_all x1, waiting for transfers between devices, shards(): lax.all_to_all(state, 'mode', split_axis=1, concat_axis=1, tiled=True)  25.8 us
  transfers between devices with their start and end apart: 4, of which 4 were waited for; matrix products, arithmetic and copies ran while one was open for 4% of the time, Pallas kernels for 0%

commit v1 on v0

--- a/solution.py
+++ b/solution.py
@@ -180,7 +180,7 @@
 
 
 UNROLL = 8
-CHAINS = 1
+MESH = pl.DeviceIdType.MESH
 
 
 def split(value):
@@ -199,12 +199,8 @@
     return dot(left[0], right[0]) + (dot(left[0], right[1]) + dot(left[1], right[0]))
 
 
-def spectral_kernel(x_ref, m1h, m1l, m2h, m2l, twist_ref, rotor_ref, out_ref):
+def transform(real, imag, m1, m2, twist_ref, ro_re, ro_im):
     radix = twist_ref.shape[1]
-    m1 = (m1h[...], m1l[...])
-    m2 = (m2h[...], m2l[...])
-    real = x_ref[:, 0, 0].reshape(radix, radix)
-    imag = x_ref[:, 1, 0].reshape(radix, radix)
     head = product(m1, split(jnp.concatenate([real, imag], axis=0)))
     head_re, head_im = head[:radix], head[radix:]
     tw_re, tw_im = twist_ref[0], twist_ref[1]
@@ -212,7 +208,6 @@
     im = head_re * tw_im + head_im * tw_re
     spec = product(split(jnp.concatenate([re, im], axis=1)), m2)
     spec_re, spec_im = spec[:, :radix], spec[:, radix:]
-    ro_re, ro_im = rotor_ref[0, 0], rotor_ref[1, 0]
     re = spec_re * ro_re - spec_im * ro_im
     im = spec_re * ro_im + spec_im * ro_re
     back = product(split(jnp.concatenate([re, im], axis=1)), m1)
@@ -220,104 +215,319 @@
     re = back_re * tw_re + back_im * tw_im
     im = back_im * tw_re - back_re * tw_im
     out = product(m2, split(jnp.concatenate([re, im], axis=0)))
-    shape = out_ref.shape[:1] + out_ref.shape[3:]
-    out_ref[:, 0, 0] = out[:radix].reshape(shape)
-    out_ref[:, 1, 0] = out[radix:].reshape(shape)
-
-
-def spectral(x, tables, twist, rotor, blocks):
-    count, _, modes, rows, radix = x.shape
-    whole = lambda a: pl.BlockSpec(a.shape, lambda g: (0,) * a.ndim)
-    return pl.pallas_call(
-        spectral_kernel,
-        grid=(modes,),
-        in_specs=[pl.BlockSpec((count, 2, 1, rows, radix), lambda g: (0, 0, g, 0, 0))]
-        + [whole(t) for t in tables]
-        + [whole(twist), pl.BlockSpec((2, 1, radix, radix), lambda g: (0, g, 0, 0))],
-        out_specs=pl.BlockSpec((blocks, 2, 1, radix // blocks, radix), lambda g: (0, 0, g, 0, 0)),
-        out_shape=jax.ShapeDtypeStruct((blocks, 2, modes, radix // blocks, radix), jnp.float32),
-        compiler_params=pltpu.CompilerParams(vmem_limit_bytes=48 * 1024 * 1024),
-        name="spectral",
-    )(x, *tables, twist, rotor)
-
-
-def kerr_kernel(stride, quartets, weights, lin_ref, out_ref, err_ref, mid_ref, *accs):
-    chains = len(accs) // 2
-    count = weights.shape[0]
+    return out[:radix], out[radix:]
+
+
+def step_kernel(
+    ways, own, index_ref, last_ref, weight_ref, keep_ref, has_ref,
+    x_ref, m1h, m1l, m2h, m2l, twist_ref, rotor_ref,
+    out_ref, err_ref,
+    sent, held_00, held_01, held_10, held_11, mid, first, partial, updated, back, final, sums, norm, norms,
+    send_sems, recv_sems,
+):
+    mode_ways, tm_ways = ways
+    devices = mode_ways * tm_ways
+    planes = 2 * own
+    held = ((held_00, held_01), (held_10, held_11))
+    my_mode, my_tm = lax.axis_index("mode"), lax.axis_index("tm")
+    me = my_tm * mode_ways + my_mode
+    radix = twist_ref.shape[1]
+    half = radix // 2
+    count = weight_ref.shape[0]
     unroll = UNROLL if count % UNROLL == 0 else 1
 
-    def evaluate(src, totals):
-        for total in totals:
-            total[...] = jnp.zeros_like(total)
-
+    def partner(k):
+        tm = lax.rem(my_tm + lax.rem(k, tm_ways), tm_ways)
+        mode = lax.rem(my_mode + k // tm_ways, mode_ways)
+        return mode, tm, tm * mode_ways + mode
+
+    barrier = pltpu.get_barrier_semaphore()
+
+    def greet(k, carry):
+        mode, tm, _ = partner(k)
+        pl.semaphore_signal(barrier, inc=1, device_id=(mode, tm), device_id_type=MESH)
+        return carry
+
+    lax.fori_loop(1, devices, greet, 0)
+
+    def to_all(pick_src, dst, slot):
+        def one(k, carry):
+            mode, tm, holder = partner(k)
+            pltpu.make_async_remote_copy(
+                src_ref=pick_src(holder),
+                dst_ref=dst,
+                send_sem=send_sems.at[slot],
+                recv_sem=recv_sems.at[slot],
+                device_id=(mode, tm),
+                device_id_type=MESH,
+            ).start()
+            return carry
+
+        lax.fori_loop(1, devices, one, 0)
+
+    def arrived(ref, slot):
+        pltpu.make_async_copy(ref, ref, recv_sems.at[slot]).wait()
+
+    def drained(ref, slot):
+        pltpu.make_async_copy(ref, ref, send_sems.at[slot]).wait()
+
+    def spectral(load, step, base):
+        m1, m2 = (m1h[...], m1l[...]), (m2h[...], m2l[...])
+
+        def one(g, carry):
+            real, imag = load(g)
+            re, im = transform(real, imag, m1, m2, twist_ref, rotor_ref[0, g], rotor_ref[1, g])
+            for part, value in enumerate((re, im)):
+                for h in range(2):
+                    piece = value[:, h * half : (h + 1) * half].reshape(devices, 8, half)
+                    sent[step, h, :, 2 * g + part] = piece
+            if step == 0:
+                @pl.when(g == 0)
+                def _():
+                    pl.semaphore_wait(barrier, devices - 1)
+            for h in range(2):
+                pair = sent[step, h, me, pl.ds(2 * g, 2)]
+                held[step][h][pl.ds(me * planes + 2 * g, 2)] = pair
+            to_all(
+                lambda holder: sent.at[step, 0, holder, pl.ds(2 * g, 2)],
+                held[step][0].at[pl.ds(me * planes + 2 * g, 2)],
+                base,
+            )
+            return carry
+
+        lax.fori_loop(0, own, one, 0)
+        to_all(
+            lambda holder: sent.at[step, 1, holder],
+            held[step][1].at[pl.ds(me * planes, planes)],
+            base + 1,
+        )
+
+    def evaluate(load):
         def chunk(c, carry):
-            pending = []
+            acc_re, acc_im = carry
             for u in range(unroll):
                 q = c * unroll + u
-                l, m, n = quartets[4 * q + 1], quartets[4 * q + 2], quartets[4 * q + 3]
-                w = weights[q]
+                l, m, n = index_ref[0, q], index_ref[1, q], index_ref[2, q]
+                w, keep = weight_ref[q], keep_ref[q]
                 re, im = triple_product(
-                    (src[l], src[l + stride]), (src[m], src[m + stride]), (src[n], src[n + stride])
+                    (load(l), load(l + 1)), (load(m), load(m + 1)), (load(n), load(n + 1))
                 )
-                pending.append((quartets[4 * q], -w * im, w * re))
-            for u, (p, re, im) in enumerate(pending):
-                total = totals[u % chains]
-                total[p] += re
-                total[p + stride] += im
+                acc_re = keep * acc_re - w * im
+                acc_im = keep * acc_im + w * re
+                partial[q, 0] = acc_re
+                partial[q, 1] = acc_im
+            return acc_re, acc_im
+
+        zero = jnp.zeros((8, half), jnp.float32)
+        lax.fori_loop(0, count // unroll, chunk, (zero, zero))
+
+    def kerr(step, h, store):
+        evaluate(lambda i: held[step][h][i])
+
+        def combine(d, carry):
+            for g in range(own):
+                row = d * own + g
+                place, has = last_ref[row], has_ref[row]
+                for r in range(2):
+                    i = d * planes + 2 * g + r
+                    value = has * partial[place, r]
+                    first[i] = value
+                    mid[i] = held[step][h][i] + value
             return carry
 
-        lax.fori_loop(0, count // unroll, chunk, 0)
-
-    evaluate(lin_ref, accs[:chains])
-    first_ref = accs[0]
-
-    def combine(i, carry):
-        first_ref[i] = sum(total[i] for total in accs[:chains])
-        mid_ref[i] = lin_ref[i] + first_ref[i]
-        return carry
-
-    lax.fori_loop(0, lin_ref.shape[0], combine, 0, unroll=4)
-    evaluate(mid_ref, accs[chains:])
-
-    def finish(i, carry):
-        first, second = first_ref[i], sum(total[i] for total in accs[chains:])
-        new = lin_ref[i] + 0.5 * (first + second)
-        estimate = 0.5 * (second - first)
-        out_ref[i] = new
-        err_ref[0, pl.ds(i, 1)] = jnp.sum(estimate * estimate, axis=0, keepdims=True)
-        err_ref[1, pl.ds(i, 1)] = jnp.sum(new * new, axis=0, keepdims=True)
-        return carry
-
-    lax.fori_loop(0, lin_ref.shape[0], finish, 0, unroll=4)
-
-
-def kerr(lin, quartets, weights, stride):
-    planes, rows, lanes = lin.shape
+        lax.fori_loop(0, devices, combine, 0)
+        evaluate(lambda i: mid[i])
+
+        def finish(d, carry):
+            for g in range(own):
+                row = d * own + g
+                place, has = last_ref[row], has_ref[row]
+                squares = [0.0, 0.0]
+                for r in range(2):
+                    i = d * planes + 2 * g + r
+                    second = has * partial[place, r]
+                    new = held[step][h][i] + 0.5 * (first[i] + second)
+                    estimate = 0.5 * (second - first[i])
+                    store(d, 2 * g + r, new)
+                    squares[0] += estimate * estimate
+                    squares[1] += new * new
+                for kind in range(2):
+                    total = jnp.sum(squares[kind], axis=0, keepdims=True)
+                    if h == 0:
+                        sums[kind, pl.ds(row, 1)] = total
+                    else:
+                        sums[kind, pl.ds(row, 1)] += total
+            return carry
+
+        lax.fori_loop(0, devices, finish, 0)
+
+    def fold(step):
+        for kind in range(2):
+            norm[pl.ds(2 * step + kind, 1)] = jnp.sum(sums[kind].T, axis=0, keepdims=True)
+
+    norm[...] = jnp.zeros_like(norm)
+    spectral(lambda g: (x_ref[:, 0, g].reshape(radix, radix), x_ref[:, 1, g].reshape(radix, radix)), 0, 0)
+
+    def keep_update(h):
+        def store(d, plane, value):
+            updated[h, d, plane] = value
+
+        return store
+
+    arrived(held[0][0].at[pl.ds(0, (devices - 1) * planes)], 0)
+    kerr(0, 0, keep_update(0))
+    back[0, me] = updated[0, me]
+    to_all(lambda holder: updated.at[0, holder], back.at[0, me], 2)
+    arrived(held[0][1].at[pl.ds(0, (devices - 1) * planes)], 1)
+    kerr(0, 1, keep_update(1))
+    back[1, me] = updated[1, me]
+    for g in range(own):
+        to_all(
+            lambda holder: updated.at[1, holder, pl.ds(2 * g, 2)],
+            back.at[1, me, pl.ds(2 * g, 2)],
+            3 + g,
+        )
+    fold(0)
+    arrived(back.at[0, pl.ds(0, devices - 1)], 2)
+
+    def load_back(g):
+        arrived(back.at[1, pl.ds(0, devices - 1), pl.ds(0, 2)], 3 + g)
+        parts = []
+        for r in range(2):
+            parts.append(
+                jnp.concatenate(
+                    [back[h, :, 2 * g + r].reshape(radix, half) for h in range(2)], axis=1
+                )
+            )
+        return parts
+
+    base = 3 + own
+    spectral(load_back, 1, base)
+
+    def last_update(h):
+        def store(d, plane, value):
+            final[h, d // mode_ways, lax.rem(d, mode_ways), plane] = value
+
+        return store
+
+    def home(h, slot):
+        def one(k, carry):
+            mode = lax.rem(my_mode + k, mode_ways)
+            pltpu.make_async_remote_copy(
+                src_ref=final.at[h, :, mode],
+                dst_ref=out_ref.at[h, my_mode],
+                send_sem=send_sems.at[slot],
+                recv_sem=recv_sems.at[slot],
+                device_id=(mode, my_tm),
+                device_id_type=MESH,
+            ).start()
+            return carry
+
+        lax.fori_loop(1, mode_ways, one, 0)
+        out_ref[h, my_mode] = final[h, :, my_mode]
+
+    for h in range(2):
+        arrived(held[1][h].at[pl.ds(0, (devices - 1) * planes)], base + h)
+        kerr(1, h, last_update(h))
+        home(h, base + 2 + h)
+    fold(1)
+    norms[me] = norm[...]
+    to_all(lambda holder: norm, norms.at[me], base + 4)
+    arrived(norms.at[pl.ds(0, devices - 1)], base + 4)
+    total = jnp.sum(norms[...], axis=0)
+    err_ref[...] = jnp.concatenate(
+        [
+            jnp.sqrt(total[2 * s : 2 * s + 1] / (total[2 * s + 1 : 2 * s + 2] + epsilon))
+            for s in range(STEPS)
+        ],
+        axis=0,
+    )
+    for h in range(2):
+        arrived(out_ref.at[h, pl.ds(0, mode_ways - 1)], base + 2 + h)
+    for step, at in ((0, 0), (1, base)):
+        for h in range(2):
+            drained(sent.at[step, h, pl.ds(0, devices - 1)], at + h)
+    drained(updated.at[0, pl.ds(0, devices - 1)], 2)
+    for g in range(own):
+        drained(updated.at[1, pl.ds(0, devices - 1), pl.ds(0, 2)], 3 + g)
+    for h in range(2):
+        drained(out_ref.at[h, pl.ds(0, mode_ways - 1)], base + 2 + h)
+    drained(norms.at[pl.ds(0, devices - 1)], base + 4)
+
+
+def step_all(ways, own, scalars, x, tables, twist, rotor):
+    mode_ways, tm_ways = ways
+    devices = mode_ways * tm_ways
+    planes = 2 * own
+    count = scalars[2].shape[0]
+    half = twist.shape[1] // 2
     vmem = pl.BlockSpec(memory_space=pltpu.VMEM)
     smem = pl.BlockSpec(memory_space=pltpu.SMEM)
+    real = lambda *shape: pltpu.VMEM(shape, jnp.float32)
+    slots = 8 + own
     return pl.pallas_call(
-        functools.partial(kerr_kernel, stride),
-        in_specs=[smem, smem, vmem],
+        functools.partial(step_kernel, ways, own),
+        in_specs=[smem] * 5 + [vmem] * 7,
         out_specs=[vmem, vmem],
         out_shape=[
-            jax.ShapeDtypeStruct(lin.shape, jnp.float32),
-            jax.ShapeDtypeStruct((2, planes, lanes), jnp.float32),
+            jax.ShapeDtypeStruct((2, mode_ways, tm_ways, planes, 8, half), jnp.float32),
+            jax.ShapeDtypeStruct((STEPS, devices * own), jnp.float32),
         ],
-        scratch_shapes=[pltpu.VMEM(lin.shape, jnp.float32)] * (1 + 2 * CHAINS),
-        compiler_params=pltpu.CompilerParams(vmem_limit_bytes=40 * 1024 * 1024),
-        name="kerr",
-    )(quartets, weights, lin)
+        scratch_shapes=[
+            real(2, 2, devices, planes, 8, half),
+            *[real(devices * planes, 8, half)] * 4,
+            real(devices * planes, 8, half),
+            real(devices * planes, 8, half),
+            real(count, 2, 8, half),
+            real(2, devices, planes, 8, half),
+            real(2, devices, planes, 8, half),
+            real(2, tm_ways, mode_ways, planes, 8, half),
+            real(2, devices * own, half),
+            real(8, devices * own),
+            real(devices, 8, devices * own),
+            pltpu.SemaphoreType.DMA((slots,)),
+            pltpu.SemaphoreType.DMA((slots,)),
+        ],
+        compiler_params=pltpu.CompilerParams(
+            vmem_limit_bytes=56 * 1024 * 1024, collective_id=0, has_side_effects=True
+        ),
+        name="step_all",
+    )(*scalars, x, *tables, twist, rotor)
+
+
+def sorted_quartets(ways, own, quartets, intersections):
+    mode_ways, tm_ways = ways
+    modes_local = own * tm_ways
+    modes_all = modes_local * mode_ways
+    row = (quartets % modes_local // own * mode_ways + quartets // modes_local) * own
+    row = row + quartets % own
+    count = row.shape[1]
+    place = lax.iota(jnp.int32, count)
+    key = row[0] * count + place
+    rank = jnp.sum((key[None, :] < key[:, None]).astype(jnp.int32), axis=1)
+    pick = (rank[None, :] == place[:, None]).astype(jnp.float32)
+    columns = jnp.concatenate([row.astype(jnp.float32), intersections[None]], axis=0)
+    ordered = contract("iq,cq->ci", pick, columns)
+    rows = jnp.round(ordered[:4]).astype(jnp.int32)
+    keep = jnp.concatenate([jnp.zeros(1, bool), rows[0, 1:] == rows[0, :-1]])
+    modes = lax.iota(jnp.int32, modes_all)
+    below = jnp.sum((row[0][None, :] <= modes[:, None]).astype(jnp.int32), axis=1)
+    has = jnp.any(row[0][None, :] == modes[:, None], axis=1)
+    return (
+        rows[1:] * 2,
+        jnp.maximum(below - 1, 0),
+        ordered[4],
+        keep.astype(jnp.float32),
+        has.astype(jnp.float32),
+    )
 
 
 def shards(ways, field, beta, quartets, intersections):
     mode_ways, tm_ways = ways
-    devices = mode_ways * tm_ways
     _, modes_local, time_local = field.shape
     total_time = time_local * tm_ways
     radix = math.isqrt(total_time)
     own = modes_local // tm_ways
-    modes_all = modes_local * mode_ways
-    rows = radix // devices
     tm_index = lax.axis_index("tm")
 
     table_re, table_im = dft_tables(radix)
@@ -344,35 +554,16 @@
         mine[0][:, None, None], mine[1][:, None, None], mine[2][:, None, None], frequency[None]
     )
     rotor = jnp.stack([jnp.cos(phase), jnp.sin(phase)]) * (1.0 / total_time)
-
-    holder = quartets % modes_local // own * mode_ways + quartets // modes_local
-    planes = (holder * (2 * own) + quartets % own).T.reshape(-1)
+    scalars = sorted_quartets(ways, own, quartets, intersections)
 
     state = field.reshape(2, tm_ways, own, time_local // radix, radix).transpose(1, 0, 2, 3, 4)
     state = lax.all_to_all(state, "tm", split_axis=0, concat_axis=0, tiled=True)
-    sums = []
-    for step_index in range(STEPS):
-        state = spectral(state, tables, twist, rotor, devices)
-        state = lax.all_to_all(state, ("tm", "mode"), split_axis=0, concat_axis=0, tiled=True)
-        flat, part = kerr(
-            state.reshape(2 * modes_all, rows, radix), planes, intersections, own
-        )
-        sums.append(part)
-        state = flat.reshape(devices, 2, own, rows, radix)
-        if step_index < STEPS - 1:
-            state = lax.all_to_all(state, ("tm", "mode"), split_axis=0, concat_axis=0, tiled=True)
-    state = state.reshape(tm_ways, mode_ways, 2, own, rows, radix)
-    state = lax.all_to_all(state, "mode", split_axis=1, concat_axis=1, tiled=True)
-    out = state.transpose(2, 0, 3, 1, 4, 5).reshape(2, modes_local, time_local)
-
-    norms = jnp.sum(jnp.stack(sums), axis=-1).reshape(STEPS, 2, tm_ways, mode_ways, 2, own)
-    norms = jnp.sum(norms, axis=4).transpose(3, 0, 1, 2, 4).reshape(mode_ways, -1)
-    norms = jnp.broadcast_to(norms[:, None], (mode_ways, tm_ways, norms.shape[1]))
-    norms = norms.reshape(devices, 1, -1)
-    norms = lax.all_to_all(norms, ("mode", "tm"), split_axis=0, concat_axis=0, tiled=True)
-    norms = jnp.sum(norms, axis=0).reshape(STEPS, 2, modes_local)
-    errors = jnp.sqrt(norms[:, 0] / (norms[:, 1] + epsilon))
-    return (out, errors)
+    out, errors = step_all(ways, own, scalars, state, tables, twist, rotor)
+    out = out.reshape(2, mode_ways, tm_ways, own, 2, 8, radix // 2)
+    out = out.transpose(4, 2, 3, 1, 5, 0, 6).reshape(2, modes_local, time_local)
+    errors = errors.reshape(STEPS, tm_ways, mode_ways, own)
+    errors = lax.dynamic_index_in_dim(errors, lax.axis_index("mode"), axis=2, keepdims=False)
+    return (out, errors.reshape(STEPS, modes_local))
 
 
 def solution(mesh):
@@ -381,7 +572,9 @@
     def body(field, beta, quartets, intersections):
         mode_ways, tm_ways = mesh.shape["mode"], mesh.shape["tm"]
         devices = mode_ways * tm_ways
-        if field.shape[1] % tm_ways == 0 and RADIX % (8 * devices) == 0:
+        total_time = field.shape[2] * tm_ways
+        fits = field.shape[1] % tm_ways == 0 and RADIX == 8 * devices
+        if fits and total_time == RADIX * RADIX and field.shape[1] * mode_ways == 128:
             return shards((mode_ways, tm_ways), field, beta, quartets, intersections)
         return shards_general(field, beta, quartets, intersections)
 

time: 327 us -> 248 us (0.76)
  Pallas kernels: 63.6 us -> 178 us
  blocking collectives: 105 us -> 0 us
  waiting for transfers between devices: 117 us -> 31.4 us
  starting transfers between devices: 17.3 us -> 6.48 us
  other arithmetic: 9.83 us -> 14.1 us
    pallas_call x4 -> x1, Pallas kernels: 63.6 us -> 178 us  [step_all(): pl.pallas_call(functools.partial(step_kernel, ways, own), in_specs=[smem]...]
    all_to_all x2 -> x0, blocking collectives: 105 us -> none  [shards(): lax.all_to_all(state, ('tm', 'mode'), split_axis=0, concat_axis=0, tiled=...]
    all_to_all x3 -> x0, waiting for transfers between devices: 77.9 us -> none  [the longest x1 46.3 us: shards(): lax.all_to_all(state, ('tm', 'mode'), split_axis=0, concat_axis=0, tiled=...]
    all_to_all x3 -> x0, starting transfers between devices: 11 us -> none  [the longest x1 3.71 us: shards(): lax.all_to_all(state, ('tm', 'mode'), split_axis=0, concat_axis=0, tiled=...]
    all_to_all x1, waiting for transfers between devices: 39.4 us -> 31.4 us  [shards(): state = lax.all_to_all(state, 'tm', split_axis=0, concat_axis=0, tiled=True)]
  transfers between devices with their start and end apart: 4 -> 1, of which waited for: 4 -> 1; matrix products, arithmetic and copies ran while one was open for 4% -> 7% of each run, Pallas kernels for 0% -> 0%
where the time goes in v1:
time: 248 us; the launch traced here: 245 us
  Pallas kernels  178 us (72%)
  waiting for transfers between devices  31.4 us (13%)
  other arithmetic  14.1 us (6%)
  local copies, waits for them, and re-layouts  12.5 us (5%)
  starting transfers between devices  6.48 us (3%)
    pallas_call x1, Pallas kernels, step_all(): pl.pallas_call(functools.partial(step_kernel, ways, own), in_specs=[smem]...  178 us
    all_to_all x1, waiting for transfers between devices, shards(): state = lax.all_to_all(state, 'tm', split_axis=0, concat_axis=0, tiled=True)  31.4 us
    all_to_all x1, starting transfers between devices, shards(): state = lax.all_to_all(state, 'tm', split_axis=0, concat_axis=0, tiled=True)  6.48 us
  transfers between devices with their start and end apart: 1, of which 1 were waited for; matrix products, arithmetic and copies ran while one was open for 7% of the time, Pallas kernels for 0%

profile of v1, /device:TPU:0, one launch (start us, length us, event | category | flops | bytes accessed | tf_op | source)
XLA Modules:
  0.0 245.2 jit_solution(7406355527618650594)
XLA Ops:
  0.6 0.0 copy-start
  0.6 2.2 copy.12
  2.9 1.5 copy.14
  4.4 0.0 copy-start.2
  4.4 0.0 copy-start.4
  4.4 6.5 %all-to-all-start = ((f32[4,2,4,64,256]{4,3,2,1,0:T(8,128)}), f32[4,2,4,64,256]{4,3,2,1,0:T(8,128)S(1)}, u32[]{:S(2)}, u32[]{:S(2)}) async-start(f32[4,2,4,64,256]{4,3,2,1,0:T(8,128)} %bitcast.20), calls=%async_computation | async-start | bytes 4194304 | tf_op jit(solution)/shard_map/all_to_all | solution.py:560
  10.9 0.0 copy-done.2
  10.9 0.1 fusion.41
  11.0 0.6 convert_reduce_fusion
  11.6 0.0 copy-done.4
  11.6 1.9 fusion
  13.5 0.6 slice.41
  14.1 0.1 fusion.8
  14.3 0.5 convert_element_type.80.has_ref
  14.8 0.0 copy-done
  14.8 0.1 constant_dynamic-slice_fusion
  14.9 0.1 compare_reduce_fusion
  15.0 0.7 add_convert_fusion.keep_ref
  15.7 0.1 convert_reduce_fusion.1
  15.8 1.0 fusion.27
  16.8 1.0 fusion.25
  17.8 1.0 fusion.23
  18.9 0.8 pad_maximum_fusion.4.twist_ref
  19.7 0.1 fusion.16
  19.8 3.8 %fusion.7 = (f32[1,4,256,256]{3,2,1,0:T(8,128)S(1)}, f32[1,4,256,256]{3,2,1,0:T(8,128)S(1)}) fusion(f32[4]{0:T(128)S(1)} %get-tuple-element.17, f32[256,256]{1,0:T(8,128)S(1)} %fusion.16, f32[4]{0:T(128)S(1)} %get-tuple-element.18, f32[4]{0:T(128)S(1)} %get-tuple-element.16), kind=kLoop, calls=%fused_computation.20 | loop fusion | flops 1310720 | bytes 2359344 | tf_op jit(solution)/shard_map/cos | solution.py:556
  23.6 1.5 maximum_multiply_fusion.rotor_ref
  25.1 1.5 fusion.5
  26.6 0.5 add_maximum_fusion.last_ref
  27.1 0.6 slice_multiply_fusion.index_ref
  27.7 31.4 %all-to-all-done.x_ref = f32[4,2,4,64,256]{4,3,2,1,0:T(8,128)S(1)} async-done(((f32[4,2,4,64,256]{4,3,2,1,0:T(8,128)}), f32[4,2,4,64,256]{4,3,2,1,0:T(8,128)S(1)}, u32[]{:S(2)}, u32[]{:S(2)}) %all-to-all-start) | async-done | bytes 2097184 | tf_op jit(solution)/shard_map/all_to_all | solution.py:560
  59.1 0.0 copy-start.1
  59.1 1.3 copy-done.1
  60.4 178.0 %step_all.1 = (f32[2,8,4,8,8,128]{5,4,3,2,1,0:T(8,128)}, f32[2,128]{1,0:T(2,128)}) custom-call(s32[3,1024]{1,0:T(4,128)} %slice_multiply_fusion.index_ref, s32[128]{0:T(128)} %add_maximum_fusion.last_ref, f32[1024]{0:T(1024)} %bitcast.28, f32[1024]{0:T(1024)} %add_convert_fusion.keep_ref, f32[128]{0:T(128)} %convert_element_type.80.has_ref, ...), custom_call_target="tpu_custom_call" | custom-call | tf_op jit(solution)/shard_map/step_all/pallas_call | solution.py:468
  238.5 3.2 %copy.11 = f32[2,4,4,8,8,2,128]{6,5,4,3,2,1,0:T(2,128)S(1)} copy(f32[2,4,4,8,8,2,128]{6,4,0,2,1,3,5:T(8,128)} %bitcast.23) | data formatting | bytes 4194304 | tf_op jit(solution)/shard_map/transpose | solution.py:563
  241.7 0.0 copy-start.3
  241.7 2.7 %reshape.180 = f32[2,16,16384]{2,1,0:T(8,128)} reshape(f32[2,4,4,8,8,2,128]{6,5,4,3,2,1,0:T(2,128)S(1)} %copy.11) | data formatting | bytes 4194304 | tf_op jit(solution)/shard_map/reshape | solution.py:563
  244.4 0.0 copy-done.3
  244.4 0.1 reshape.181
  244.5 0.6 reshape.182
  (6 shorter events, 0.1 us)
Async XLA Ops:
  0.6 14.2 %copy-start = (f32[3,16]{1,0:T(4,128)S(1)}, f32[3,16]{1,0:T(4,128)}, u32[]{:S(2)}) copy-start(f32[3,16]{1,0:T(4,128)} %param.5) | copy-start | bytes 580
  4.4 6.5 %copy-start.2 = (s32[4,1024]{1,0:T(4,128)S(1)}, s32[4,1024]{1,0:T(4,128)}, u32[]{:S(2)}) copy-start(s32[4,1024]{1,0:T(4,128)} %param.6) | copy-start | bytes 49156
  4.4 7.1 %copy-start.4 = (f32[1024]{0:T(1024)S(1)}, f32[1024]{0:T(1024)}, u32[]{:S(2)}) copy-start(f32[1024]{0:T(1024)} %param.7) | copy-start | bytes 12292
  4.4 54.7 %all-to-all-start = ((f32[4,2,4,64,256]{4,3,2,1,0:T(8,128)}), f32[4,2,4,64,256]{4,3,2,1,0:T(8,128)S(1)}, u32[]{:S(2)}, u32[]{:S(2)}) async-start(f32[4,2,4,64,256]{4,3,2,1,0:T(8,128)} %bitcast.20), calls=%async_computation | async-start | bytes 4194304 | tf_op jit(solution)/shard_map/all_to_all | solution.py:560
  59.1 1.3 copy-start.1
  241.7 2.7 %copy-start.3 = (f32[2,128]{1,0:T(2,128)S(1)}, f32[2,128]{1,0:T(2,128)}, u32[]{:S(2)}) copy-start(f32[2,128]{1,0:T(2,128)} %get-tuple-element.5) | copy-start | bytes 3076

commit v2 on v1

--- a/solution.py
+++ b/solution.py
@@ -3,6 +3,7 @@
 
 import jax
 import jax.numpy as jnp
+import numpy as np
 from jax import lax
 from jax.experimental import pallas as pl
 from jax.experimental.pallas import tpu as pltpu
@@ -183,6 +184,16 @@
 MESH = pl.DeviceIdType.MESH
 
 
+def half_pi_terms():
+    whole = math.pi / 2
+    first = math.floor(whole * 2**11) / 2**11
+    second = math.floor((whole - first) * 2**23) / 2**23
+    return first, second, whole - first - second
+
+
+HALF_PI = half_pi_terms()
+
+
 def split(value):
     high = value.astype(jnp.bfloat16)
     low = (value - high.astype(jnp.float32)).astype(jnp.bfloat16)
@@ -218,12 +229,32 @@
     return out[:radix], out[radix:]
 
 
+def cos_sin(angle):
+    turns = jnp.round(angle * (2.0 / math.pi))
+    rest = angle - turns * HALF_PI[0]
+    rest = rest - turns * HALF_PI[1]
+    rest = rest - turns * HALF_PI[2]
+    square = rest * rest
+    sine = -1.9515295891e-4 * square + 8.3321608736e-3
+    sine = (sine * square - 1.6666654611e-1) * square * rest + rest
+    cosine = 2.443315711809948e-5 * square - 1.388731625493765e-3
+    cosine = (cosine * square + 4.166664568298827e-2) * square * square - 0.5 * square + 1.0
+    quarter = turns.astype(jnp.int32)
+    odd = (quarter & 1) == 1
+    cos_part = jnp.where(odd, sine, cosine)
+    sin_part = jnp.where(odd, cosine, sine)
+    cos_part = jnp.where(((quarter + 1) & 2) == 2, -cos_part, cos_part)
+    sin_part = jnp.where((quarter & 2) == 2, -sin_part, sin_part)
+    return cos_part, sin_part
+
+
 def step_kernel(
-    ways, own, index_ref, last_ref, weight_ref, keep_ref, has_ref,
-    x_ref, m1h, m1l, m2h, m2l, twist_ref, rotor_ref,
+    ways, own, beta_ref, quartets_ref, intersections_ref, x_ref, table_ref, twist_ref,
     out_ref, err_ref,
+    m1h, m1l, m2h, m2l, rotor_ref, staged, columns,
     sent, held_00, held_01, held_10, held_11, mid, first, partial, updated, back, final, sums, norm, norms,
-    send_sems, recv_sems,
+    places, shares, spread_ref, weight_ref, keep_ref, left_ref, middle_ref, right_ref, last_ref, has_ref,
+    send_sems, recv_sems, table_sems,
 ):
     mode_ways, tm_ways = ways
     devices = mode_ways * tm_ways
@@ -234,7 +265,12 @@
     radix = twist_ref.shape[1]
     half = radix // 2
     count = weight_ref.shape[0]
+    modes_local = own * tm_ways
     unroll = UNROLL if count % UNROLL == 0 else 1
+    total_time = radix * radix
+    rows_local = radix // tm_ways
+    head = 8 + own
+    octets = x_ref.shape[1]
 
     def partner(k):
         tm = lax.rem(my_tm + lax.rem(k, tm_ways), tm_ways)
@@ -275,16 +311,14 @@
         m1, m2 = (m1h[...], m1l[...]), (m2h[...], m2l[...])
 
         def one(g, carry):
+            if step == 0:
+                make_rotor(g)
             real, imag = load(g)
             re, im = transform(real, imag, m1, m2, twist_ref, rotor_ref[0, g], rotor_ref[1, g])
             for part, value in enumerate((re, im)):
                 for h in range(2):
                     piece = value[:, h * half : (h + 1) * half].reshape(devices, 8, half)
                     sent[step, h, :, 2 * g + part] = piece
-            if step == 0:
-                @pl.when(g == 0)
-                def _():
-                    pl.semaphore_wait(barrier, devices - 1)
             for h in range(2):
                 pair = sent[step, h, me, pl.ds(2 * g, 2)]
                 held[step][h][pl.ds(me * planes + 2 * g, 2)] = pair
@@ -302,16 +336,77 @@
             base + 1,
         )
 
-    def evaluate(load):
+    def order_quartets():
+        quartet = quartets_ref[...]
+        row = (quartet % modes_local // own * mode_ways + quartet // modes_local) * own
+        row = row + quartet % own
+        position = lax.broadcasted_iota(jnp.int32, (1, count), 1)
+        lane = lax.broadcasted_iota(jnp.int32, (1, half), 1)
+        spread = lambda line: jnp.broadcast_to(line, (half, count)).T
+        key = row[0:1] * count + position
+        places[4:5] = key
+        spread_ref[4] = spread(key)
+        for i in range(4):
+            spread_ref[i] = spread(row[i : i + 1])
+        weight_ref[...] = spread(intersections_ref[...])
+        gather = lambda mask, values: jnp.sum(
+            jnp.where(mask, values, jnp.zeros_like(values)), axis=0, keepdims=True
+        )
+
+        def rank_block(b, carry):
+            here = pl.ds(pl.multiple_of(b * half, half), half)
+            before = spread_ref[4] < places[4:5, here]
+            places[5:6, here] = gather(before, jnp.ones((count, half), jnp.int32))
+            return carry
+
+        lax.fori_loop(0, count // half, rank_block, 0)
+        spread_ref[4] = spread(places[5:6])
+
+        def place_block(b, carry):
+            here = pl.ds(pl.multiple_of(b * half, half), half)
+            hit = spread_ref[4] == lane + b * half
+            for i in range(4):
+                places[i : i + 1, here] = gather(hit, spread_ref[i])
+            shares[1:2, here] = gather(hit, weight_ref[...])
+            return carry
+
+        lax.fori_loop(0, count // half, place_block, 0)
+        ones = jnp.ones((count, half), jnp.int32)
+        below = gather(spread_ref[0] <= lane, ones)
+        equal = gather(spread_ref[0] == lane, ones)
+        places[4:5, :half] = jnp.maximum(below - 1, 0)
+        shares[0:1, :half] = jnp.where(equal > 0, 1.0, 0.0)
+        owner = places[0:1]
+        same = jnp.logical_and(owner == pltpu.roll(owner, 1, 1), position > 0)
+        keep_ref[...] = spread(jnp.where(same, 1.0, 0.0))
+        weight_ref[...] = spread(shares[1:2])
+        for i in range(1, 4):
+            places[i : i + 1] = places[i : i + 1] * 2
+        copies = [
+            pltpu.make_async_copy(places.at[1 + i], ref, table_sems.at[i])
+            for i, ref in enumerate((left_ref, middle_ref, right_ref))
+        ]
+        copies.append(
+            pltpu.make_async_copy(places.at[4, pl.ds(0, half)], last_ref, table_sems.at[3])
+        )
+        copies.append(pltpu.make_async_copy(shares.at[0, pl.ds(0, half)], has_ref, table_sems.at[4]))
+        for copy in copies:
+            copy.start()
+        for copy in copies:
+            copy.wait()
+
+    def evaluate(source):
+        load = lambda plane: (source[plane], source[plane + 1])
+
         def chunk(c, carry):
             acc_re, acc_im = carry
             for u in range(unroll):
                 q = c * unroll + u
-                l, m, n = index_ref[0, q], index_ref[1, q], index_ref[2, q]
-                w, keep = weight_ref[q], keep_ref[q]
                 re, im = triple_product(
-                    (load(l), load(l + 1)), (load(m), load(m + 1)), (load(n), load(n + 1))
+                    load(left_ref[q]), load(middle_ref[q]), load(right_ref[q])
                 )
+                w = jnp.broadcast_to(weight_ref[pl.ds(q, 1), :], (8, half))
+                keep = jnp.broadcast_to(keep_ref[pl.ds(q, 1), :], (8, half))
                 acc_re = keep * acc_re - w * im
                 acc_im = keep * acc_im + w * re
                 partial[q, 0] = acc_re
@@ -322,7 +417,7 @@
         lax.fori_loop(0, count // unroll, chunk, (zero, zero))
 
     def kerr(step, h, store):
-        evaluate(lambda i: held[step][h][i])
+        evaluate(held[step][h])
 
         def combine(d, carry):
             for g in range(own):
@@ -336,7 +431,7 @@
             return carry
 
         lax.fori_loop(0, devices, combine, 0)
-        evaluate(lambda i: mid[i])
+        evaluate(mid)
 
         def finish(d, carry):
             for g in range(own):
@@ -366,7 +461,70 @@
             norm[pl.ds(2 * step + kind, 1)] = jnp.sum(sums[kind].T, axis=0, keepdims=True)
 
     norm[...] = jnp.zeros_like(norm)
-    spectral(lambda g: (x_ref[:, 0, g].reshape(radix, radix), x_ref[:, 1, g].reshape(radix, radix)), 0, 0)
+    for g in range(own):
+        for t in range(tm_ways):
+            octet, line = divmod(t * own + g, 8)
+            for r in range(2):
+                for side in range(2):
+                    rows = pl.ds(line + 8 * side, rows_local, stride=16)
+                    staged[g, t, r, side] = x_ref[r, octet, rows, :]
+        if g == 0:
+            pl.semaphore_wait(barrier, devices - 1)
+        columns[g, my_tm] = staged[g, my_tm]
+
+        def fetch(k, carry, g=g):
+            tm = lax.rem(my_tm + k, tm_ways)
+            pltpu.make_async_remote_copy(
+                src_ref=staged.at[g, tm],
+                dst_ref=columns.at[g, my_tm],
+                send_sem=send_sems.at[head + g],
+                recv_sem=recv_sems.at[head + g],
+                device_id=(my_mode, tm),
+                device_id_type=MESH,
+            ).start()
+            return carry
+
+        lax.fori_loop(1, tm_ways, fetch, 0)
+
+    for part, (m1, m2) in enumerate(((m1h, m2h), (m1l, m2l))):
+        re, im = table_ref[part, 0], table_ref[part, 1]
+        for table, sign in ((m1, 1), (m2, -1)):
+            table[:radix, :radix] = re
+            table[radix:, radix:] = re
+            table[:radix, radix:] = -im if sign == 1 else im
+            table[radix:, :radix] = im if sign == 1 else -im
+
+    order_quartets()
+
+    def make_rotor(g):
+        mode = my_tm * own + g
+        offset, slope, curve = (beta_ref[i, mode] for i in range(3))
+        offset, slope, curve = math.pi * offset, 300.0 * slope, 3000.0 * curve
+
+        def strip(c, carry):
+            start = pl.multiple_of(8 * c, 8)
+            row = lax.broadcasted_iota(jnp.int32, (8, radix), 0) + start
+            wave = row + radix * lax.broadcasted_iota(jnp.int32, (8, radix), 1)
+            signed = jnp.where(wave < total_time // 2, wave, wave - total_time)
+            frequency = signed.astype(jnp.float32) * (2.0 / total_time)
+            phase = offset + slope * frequency + curve * frequency * frequency
+            cosine, sine = cos_sin(phase)
+            rotor_ref[0, g, pl.ds(start, 8)] = cosine * (1.0 / total_time)
+            rotor_ref[1, g, pl.ds(start, 8)] = sine * (1.0 / total_time)
+            return carry
+
+        lax.fori_loop(0, radix // 8, strip, 0, unroll=4)
+
+    def load_columns(g):
+        arrived(columns.at[g, pl.ds(0, tm_ways - 1)], head + g)
+        return [
+            jnp.concatenate(
+                [columns[g, :, r, side].reshape(radix, half) for side in range(2)], axis=1
+            )
+            for r in range(2)
+        ]
+
+    spectral(load_columns, 0, 0)
 
     def keep_update(h):
         def store(d, plane, value):
@@ -406,7 +564,12 @@
 
     def last_update(h):
         def store(d, plane, value):
-            final[h, d // mode_ways, lax.rem(d, mode_ways), plane] = value
+            g, r = divmod(plane, 2)
+            mode = d // mode_ways * own + g
+            rows = pl.ds(lax.rem(mode, 8), 8, stride=8)
+            final.reshape(2, mode_ways, 2, octets, 64, half)[
+                h, lax.rem(d, mode_ways), r, mode // 8, rows, :
+            ] = value
 
         return store
 
@@ -414,8 +577,8 @@
         def one(k, carry):
             mode = lax.rem(my_mode + k, mode_ways)
             pltpu.make_async_remote_copy(
-                src_ref=final.at[h, :, mode],
-                dst_ref=out_ref.at[h, my_mode],
+                src_ref=final.at[h, mode],
+                dst_ref=out_ref.at[:, :, my_mode, :, h],
                 send_sem=send_sems.at[slot],
                 recv_sem=recv_sems.at[slot],
                 device_id=(mode, my_tm),
@@ -424,7 +587,7 @@
             return carry
 
         lax.fori_loop(1, mode_ways, one, 0)
-        out_ref[h, my_mode] = final[h, :, my_mode]
+        out_ref[:, :, my_mode, :, h] = final[h, my_mode]
 
     for h in range(2):
         arrived(held[1][h].at[pl.ds(0, (devices - 1) * planes)], base + h)
@@ -435,6 +598,10 @@
     to_all(lambda holder: norm, norms.at[me], base + 4)
     arrived(norms.at[pl.ds(0, devices - 1)], base + 4)
     total = jnp.sum(norms[...], axis=0)
+    mode = lax.broadcasted_iota(jnp.int32, (devices * own, modes_local), 1)
+    place = lax.broadcasted_iota(jnp.int32, (devices * own, modes_local), 0)
+    pick = place == (mode // own * mode_ways + my_mode) * own + mode % own
+    total = contract("ij,jk->ik", total, jnp.where(pick, 1.0, 0.0))
     err_ref[...] = jnp.concatenate(
         [
             jnp.sqrt(total[2 * s : 2 * s + 1] / (total[2 * s + 1 : 2 * s + 2] + epsilon))
@@ -443,7 +610,7 @@
         axis=0,
     )
     for h in range(2):
-        arrived(out_ref.at[h, pl.ds(0, mode_ways - 1)], base + 2 + h)
+        arrived(final.at[h, pl.ds(0, mode_ways - 1)], base + 2 + h)
     for step, at in ((0, 0), (1, base)):
         for h in range(2):
             drained(sent.at[step, h, pl.ds(0, devices - 1)], at + h)
@@ -451,29 +618,37 @@
     for g in range(own):
         drained(updated.at[1, pl.ds(0, devices - 1), pl.ds(0, 2)], 3 + g)
     for h in range(2):
-        drained(out_ref.at[h, pl.ds(0, mode_ways - 1)], base + 2 + h)
+        drained(final.at[h, pl.ds(0, mode_ways - 1)], base + 2 + h)
+    for g in range(own):
+        drained(columns.at[g, pl.ds(0, tm_ways - 1)], head + g)
     drained(norms.at[pl.ds(0, devices - 1)], base + 4)
 
 
-def step_all(ways, own, scalars, x, tables, twist, rotor):
+def step_all(ways, own, beta, quartets, intersections, x, table, twist):
     mode_ways, tm_ways = ways
     devices = mode_ways * tm_ways
     planes = 2 * own
-    count = scalars[2].shape[0]
-    half = twist.shape[1] // 2
+    count = quartets.shape[1]
+    radix = twist.shape[1]
+    half = radix // 2
+    octets = x.shape[1]
     vmem = pl.BlockSpec(memory_space=pltpu.VMEM)
     smem = pl.BlockSpec(memory_space=pltpu.SMEM)
     real = lambda *shape: pltpu.VMEM(shape, jnp.float32)
-    slots = 8 + own
+    slots = 8 + 2 * own
     return pl.pallas_call(
         functools.partial(step_kernel, ways, own),
-        in_specs=[smem] * 5 + [vmem] * 7,
+        in_specs=[smem] + [vmem] * 5,
         out_specs=[vmem, vmem],
         out_shape=[
-            jax.ShapeDtypeStruct((2, mode_ways, tm_ways, planes, 8, half), jnp.float32),
-            jax.ShapeDtypeStruct((STEPS, devices * own), jnp.float32),
+            jax.ShapeDtypeStruct((2, octets, mode_ways, 8, 2, 8, half), jnp.float32),
+            jax.ShapeDtypeStruct((STEPS, own * tm_ways), jnp.float32),
         ],
         scratch_shapes=[
+            *[pltpu.VMEM((2 * radix, 2 * radix), jnp.bfloat16)] * 4,
+            real(2, own, radix, radix),
+            real(own, tm_ways, 2, 2, radix // tm_ways, half),
+            real(own, tm_ways, 2, 2, radix // tm_ways, half),
             real(2, 2, devices, planes, 8, half),
             *[real(devices * planes, 8, half)] * 4,
             real(devices * planes, 8, half),
@@ -481,89 +656,53 @@
             real(count, 2, 8, half),
             real(2, devices, planes, 8, half),
             real(2, devices, planes, 8, half),
-            real(2, tm_ways, mode_ways, planes, 8, half),
+            real(2, mode_ways, 2, octets, 8, 8, half),
             real(2, devices * own, half),
             real(8, devices * own),
             real(devices, 8, devices * own),
+            pltpu.VMEM((8, count), jnp.int32),
+            real(2, count),
+            pltpu.VMEM((5, count, half), jnp.int32),
+            real(count, half),
+            real(count, half),
+            *[pltpu.SMEM((count,), jnp.int32)] * 3,
+            pltpu.SMEM((half,), jnp.int32),
+            pltpu.SMEM((half,), jnp.float32),
             pltpu.SemaphoreType.DMA((slots,)),
             pltpu.SemaphoreType.DMA((slots,)),
+            pltpu.SemaphoreType.DMA((5,)),
         ],
         compiler_params=pltpu.CompilerParams(
             vmem_limit_bytes=56 * 1024 * 1024, collective_id=0, has_side_effects=True
         ),
         name="step_all",
-    )(*scalars, x, *tables, twist, rotor)
-
-
-def sorted_quartets(ways, own, quartets, intersections):
-    mode_ways, tm_ways = ways
-    modes_local = own * tm_ways
-    modes_all = modes_local * mode_ways
-    row = (quartets % modes_local // own * mode_ways + quartets // modes_local) * own
-    row = row + quartets % own
-    count = row.shape[1]
-    place = lax.iota(jnp.int32, count)
-    key = row[0] * count + place
-    rank = jnp.sum((key[None, :] < key[:, None]).astype(jnp.int32), axis=1)
-    pick = (rank[None, :] == place[:, None]).astype(jnp.float32)
-    columns = jnp.concatenate([row.astype(jnp.float32), intersections[None]], axis=0)
-    ordered = contract("iq,cq->ci", pick, columns)
-    rows = jnp.round(ordered[:4]).astype(jnp.int32)
-    keep = jnp.concatenate([jnp.zeros(1, bool), rows[0, 1:] == rows[0, :-1]])
-    modes = lax.iota(jnp.int32, modes_all)
-    below = jnp.sum((row[0][None, :] <= modes[:, None]).astype(jnp.int32), axis=1)
-    has = jnp.any(row[0][None, :] == modes[:, None], axis=1)
-    return (
-        rows[1:] * 2,
-        jnp.maximum(below - 1, 0),
-        ordered[4],
-        keep.astype(jnp.float32),
-        has.astype(jnp.float32),
-    )
+    )(beta, quartets, intersections[None], x, table, twist)
+
+
+def constant_tables(radix):
+    position = np.arange(radix)
+    product_of = position[:, None] * position[None, :]
+    angle = -2.0 * np.pi / radix * (product_of % radix)
+    table = np.stack([np.cos(angle), np.sin(angle)]).astype(np.float32)
+    high = table.astype(jnp.bfloat16)
+    low = (table - high.astype(np.float32)).astype(jnp.bfloat16)
+    turn = -2.0 * np.pi / radix**2 * product_of
+    twist = np.stack([np.cos(turn), np.sin(turn)]).astype(np.float32)
+    return jnp.asarray(np.stack([high, low])), jnp.asarray(twist)
 
 
 def shards(ways, field, beta, quartets, intersections):
     mode_ways, tm_ways = ways
     _, modes_local, time_local = field.shape
-    total_time = time_local * tm_ways
-    radix = math.isqrt(total_time)
+    radix = math.isqrt(time_local * tm_ways)
     own = modes_local // tm_ways
-    tm_index = lax.axis_index("tm")
-
-    table_re, table_im = dft_tables(radix)
-    m1 = jnp.concatenate(
-        [jnp.concatenate([table_re, -table_im], 1), jnp.concatenate([table_im, table_re], 1)], 0
-    )
-    m2 = jnp.concatenate(
-        [jnp.concatenate([table_re, table_im], 1), jnp.concatenate([-table_im, table_re], 1)], 0
-    )
-    tables = split_table(m1) + split_table(m2)
-    position = lax.iota(jnp.int32, radix)
-    angle = (
-        -2.0
-        * math.pi
-        / total_time
-        * (position[:, None] * position[None, :] % total_time).astype(jnp.float32)
-    )
-    twist = jnp.stack([jnp.cos(angle), jnp.sin(angle)])
-    wave = position[:, None] + radix * position[None, :]
-    signed = jnp.where(wave < total_time // 2, wave, wave - total_time)
-    frequency = signed.astype(jnp.float32) / (total_time / 2)
-    mine = lax.dynamic_slice_in_dim(beta, tm_index * own, own, axis=1)
-    phase = phase_of(
-        mine[0][:, None, None], mine[1][:, None, None], mine[2][:, None, None], frequency[None]
-    )
-    rotor = jnp.stack([jnp.cos(phase), jnp.sin(phase)]) * (1.0 / total_time)
-    scalars = sorted_quartets(ways, own, quartets, intersections)
-
-    state = field.reshape(2, tm_ways, own, time_local // radix, radix).transpose(1, 0, 2, 3, 4)
-    state = lax.all_to_all(state, "tm", split_axis=0, concat_axis=0, tiled=True)
-    out, errors = step_all(ways, own, scalars, state, tables, twist, rotor)
-    out = out.reshape(2, mode_ways, tm_ways, own, 2, 8, radix // 2)
-    out = out.transpose(4, 2, 3, 1, 5, 0, 6).reshape(2, modes_local, time_local)
-    errors = errors.reshape(STEPS, tm_ways, mode_ways, own)
-    errors = lax.dynamic_index_in_dim(errors, lax.axis_index("mode"), axis=2, keepdims=False)
-    return (out, errors.reshape(STEPS, modes_local))
+    table, twist = constant_tables(radix)
+    octets, tiles = modes_local // 8, time_local // 128
+    x = field.reshape(2, octets, 8, tiles, 128).transpose(0, 1, 3, 2, 4)
+    x = x.reshape(2, octets, tiles * 8, 128)
+    out, errors = step_all(ways, own, beta, quartets, intersections, x, table, twist)
+    out = out.reshape(2, octets, tiles, 8, 128).transpose(0, 1, 3, 2, 4)
+    return (out.reshape(2, modes_local, time_local), errors)
 
 
 def solution(mesh):
@@ -574,6 +713,7 @@
         devices = mode_ways * tm_ways
         total_time = field.shape[2] * tm_ways
         fits = field.shape[1] % tm_ways == 0 and RADIX == 8 * devices
+        fits = fits and field.shape[1] % 8 == 0 and quartets.shape[1] % 128 == 0
         if fits and total_time == RADIX * RADIX and field.shape[1] * mode_ways == 128:
             return shards((mode_ways, tm_ways), field, beta, quartets, intersections)
         return shards_general(field, beta, quartets, intersections)

time: 248 us -> 224 us (0.903); the launches traced: 245 us -> 224 us
  Pallas kernels: 178 us -> 220 us
  waiting for transfers between devices: 31.4 us -> 0 us
  other arithmetic: 14.1 us -> 0 us
  local copies, waits for them, and re-layouts: 12.5 us -> 3.61 us
  starting transfers between devices: 6.48 us -> 0 us
    pallas_call x1, Pallas kernels: 178 us -> 220 us  [step_all(): pl.pallas_call(functools.partial(step_kernel, ways, own), in_specs=[smem]...]
    all_to_all x1 -> x0, waiting for transfers between devices: 31.4 us -> none  [shards(): state = lax.all_to_all(state, 'tm', split_axis=0, concat_axis=0, tiled=True)]
    all_to_all x1 -> x0, starting transfers between devices: 6.48 us -> none  [shards(): state = lax.all_to_all(state, 'tm', split_axis=0, concat_axis=0, tiled=True)]
    reshape x4 -> x0, local copies, waits for them, and re-layouts: 4.97 us -> none  [the longest x1 2.68 us: shards(): out = out.transpose(4, 2, 3, 1, 5, 0, 6).reshape(2, modes_local, time_local)]
    cos x1 -> x0, other arithmetic: 3.83 us -> none  [shards(): rotor = jnp.stack([jnp.cos(phase), jnp.sin(phase)]) * (1.0 / total_time)]
    transpose x1 -> x0, local copies, waits for them, and re-layouts: 3.21 us -> none  [shards(): out = out.transpose(4, 2, 3, 1, 5, 0, 6).reshape(2, modes_local, time_local)]
    convert_element_type x5 -> x0, other arithmetic: 2.79 us -> none  [the longest x1 1.51 us: split_table(): return (high.astype(jnp.bfloat16), (value - high).astype(jnp.bfloat16))]
  transfers between devices with their start and end apart: 1 -> 0, of which waited for: 1 -> 0; matrix products, arithmetic and copies ran while one was open for 7% -> 0% of each run, Pallas kernels for 0% -> 0%
where the time goes in v2:
time: 224 us
  Pallas kernels  220 us (98%)
  local copies, waits for them, and re-layouts  3.61 us (2%)
    pallas_call x1, Pallas kernels, step_all(): pl.pallas_call(functools.partial(step_kernel, ways, own), in_specs=[smem]...  220 us

profile of v2, /device:TPU:0, one launch (start us, length us, event | category | flops | bytes accessed | tf_op | source)
XLA Modules:
  0.0 224.0 jit_solution(113077765484242599)
XLA Ops:
  0.6 219.7 %step_all.1 = (f32[2,2,8,8,2,8,128]{6,5,4,3,2,1,0:T(8,128)}, f32[2,16]{1,0:T(2,128)}) custom-call(f32[3,16]{1,0:T(4,128)} %beta_ref.1, s32[4,1024]{1,0:T(4,128)} %quartets_ref.1, f32[1,1024]{1,0:T(1,128)} %bitcast.13, f32[2,2,1024,128]{3,2,1,0:T(8,128)} %bitcast.11, bf16[2,2,256,256]{3,2,1,0:T(8,128)(2,1)} %constant.4.clone.table_ref, ...), custom_call_target="tpu_custom_call" | custom-call | tf_op jit(solution)/shard_map/step_all/pallas_call | solution.py:639
  220.4 0.0 copy-start
  220.4 3.0 %copy.10 = f32[2,16,16384]{2,1,0:T(8,128)} copy(f32[2,16,16384]{2,1,0:T(8,128)} %bitcast.12) | data formatting | bytes 4194304
  223.4 0.0 copy-done
  223.4 0.6 copy.11
Async XLA Ops:
  220.4 3.1 %copy-start = (f32[2,16]{1,0:T(2,128)S(1)}, f32[2,16]{1,0:T(2,128)}, u32[]{:S(2)}) copy-start(f32[2,16]{1,0:T(2,128)} %get-tuple-element.9) | copy-start | bytes 388

commit v3 on v2

--- a/solution.py
+++ b/solution.py
@@ -180,7 +180,7 @@
     return (state.reshape(2, modes_local, time_local), errors)
 
 
-UNROLL = 8
+UNROLL = 32
 MESH = pl.DeviceIdType.MESH
 
 
@@ -249,27 +249,37 @@
 
 
 def step_kernel(
-    ways, own, beta_ref, quartets_ref, intersections_ref, x_ref, table_ref, twist_ref,
+    ways, own, beta_ref, quartets_ref, intersections_ref, x_hbm, table_hbm, twist_hbm,
     out_ref, err_ref,
+    x_ref, table_ref, twist_ref,
     m1h, m1l, m2h, m2l, rotor_ref, staged, columns,
-    sent, held_00, held_01, held_10, held_11, mid, first, partial, updated, back, final, sums, norm, norms,
+    sent, short, relay, held_00, held_01, held_10, held_11, held_12, mid, first, partial, updated, back, final, sums, norm, norms,
     places, shares, spread_ref, weight_ref, keep_ref, left_ref, middle_ref, right_ref, last_ref, has_ref,
-    send_sems, recv_sems, table_sems,
+    send_sems, recv_sems, table_sems, own_sems,
 ):
     mode_ways, tm_ways = ways
     devices = mode_ways * tm_ways
     planes = 2 * own
-    held = ((held_00, held_01), (held_10, held_11))
     my_mode, my_tm = lax.axis_index("mode"), lax.axis_index("tm")
     me = my_tm * mode_ways + my_mode
     radix = twist_ref.shape[1]
     half = radix // 2
+    parts = (
+        ((sent.at[0], held_00, 0, 0, 8), (sent.at[1], held_01, 1, 0, 8)),
+        (
+            (sent.at[2], held_10, 0, 0, 8),
+            (short.at[0].reshape(devices, planes, 4, half), held_11, 1, 0, 4),
+            (short.at[1].reshape(devices, planes, 4, half), held_12, 1, 4, 4),
+        ),
+    )
     count = weight_ref.shape[0]
     modes_local = own * tm_ways
     unroll = UNROLL if count % UNROLL == 0 else 1
     total_time = radix * radix
     rows_local = radix // tm_ways
-    head = 8 + own
+    slot_back, slot_last = 2, 3 + own
+    slot_home, slot_norm, head = slot_last + 3, slot_last + 6, slot_last + 7
+    slot_relay = head + own
     octets = x_ref.shape[1]
 
     def partner(k):
@@ -285,6 +295,14 @@
         return carry
 
     lax.fori_loop(1, devices, greet, 0)
+    loads = [
+        pltpu.make_async_copy(src, dst, table_sems.at[5 + i])
+        for i, (src, dst) in enumerate(
+            ((x_hbm, x_ref), (table_hbm, table_ref), (twist_hbm, twist_ref))
+        )
+    ]
+    for copy in loads:
+        copy.start()
 
     def to_all(pick_src, dst, slot):
         def one(k, carry):
@@ -307,6 +325,43 @@
     def drained(ref, slot):
         pltpu.make_async_copy(ref, ref, send_sems.at[slot]).wait()
 
+    def to_plane(g):
+        pair = pl.ds(2 * g, 2)
+        relay[:, :, my_mode, pair] = short[:, :, my_mode, pair]
+
+        def one(k, carry):
+            mode = lax.rem(my_mode + k, mode_ways)
+            pltpu.make_async_remote_copy(
+                src_ref=short.at[:, :, mode, pair],
+                dst_ref=relay.at[:, :, my_mode, pair],
+                send_sem=send_sems.at[slot_relay + g],
+                recv_sem=recv_sems.at[slot_relay + g],
+                device_id=(mode, my_tm),
+                device_id_type=MESH,
+            ).start()
+            return carry
+
+        lax.fori_loop(1, mode_ways, one, 0)
+
+    def forward(i, slot):
+        target = parts[1][1 + i][1].reshape(devices, planes, 4, half)
+        mine = pl.ds(my_tm * mode_ways, mode_ways)
+
+        def one(k, carry):
+            tm = lax.rem(my_tm + k, tm_ways)
+            pltpu.make_async_remote_copy(
+                src_ref=relay.at[i, tm],
+                dst_ref=target.at[mine],
+                send_sem=send_sems.at[slot],
+                recv_sem=recv_sems.at[slot],
+                device_id=(my_mode, tm),
+                device_id_type=MESH,
+            ).start()
+            return carry
+
+        lax.fori_loop(1, tm_ways, one, 0)
+        target[mine] = relay[i, my_tm]
+
     def spectral(load, step, base):
         m1, m2 = (m1h[...], m1l[...]), (m2h[...], m2l[...])
 
@@ -316,24 +371,32 @@
             real, imag = load(g)
             re, im = transform(real, imag, m1, m2, twist_ref, rotor_ref[0, g], rotor_ref[1, g])
             for part, value in enumerate((re, im)):
-                for h in range(2):
+                for source, _, h, row, rows in parts[step]:
                     piece = value[:, h * half : (h + 1) * half].reshape(devices, 8, half)
-                    sent[step, h, :, 2 * g + part] = piece
-            for h in range(2):
-                pair = sent[step, h, me, pl.ds(2 * g, 2)]
-                held[step][h][pl.ds(me * planes + 2 * g, 2)] = pair
+                    source[:, 2 * g + part] = piece[:, row : row + rows]
+            direct = parts[step] if step == 0 else parts[step][:1]
+            for source, target, _, _, _ in direct:
+                target[pl.ds(me * planes + 2 * g, 2)] = source[me, pl.ds(2 * g, 2)]
+            if step == 1:
+                to_plane(g)
+            source, target = parts[step][0][:2]
             to_all(
-                lambda holder: sent.at[step, 0, holder, pl.ds(2 * g, 2)],
-                held[step][0].at[pl.ds(me * planes + 2 * g, 2)],
+                lambda holder: source.at[holder, pl.ds(2 * g, 2)],
+                target.at[pl.ds(me * planes + 2 * g, 2)],
                 base,
             )
             return carry
 
         lax.fori_loop(0, own, one, 0)
+        if step == 1:
+            for g in range(own):
+                arrived(relay.at[:, :, pl.ds(0, mode_ways - 1), pl.ds(0, 2)], slot_relay + g)
+            for i in range(2):
+                forward(i, base + 1 + i)
+            return
+        source, target = parts[step][1][:2]
         to_all(
-            lambda holder: sent.at[step, 1, holder],
-            held[step][1].at[pl.ds(me * planes, planes)],
-            base + 1,
+            lambda holder: source.at[holder], target.at[pl.ds(me * planes, planes)], base + 1
         )
 
     def order_quartets():
@@ -395,8 +458,8 @@
         for copy in copies:
             copy.wait()
 
-    def evaluate(source):
-        load = lambda plane: (source[plane], source[plane + 1])
+    def evaluate(source, rows):
+        load = lambda plane: (source[plane, :rows], source[plane + 1, :rows])
 
         def chunk(c, carry):
             acc_re, acc_im = carry
@@ -405,19 +468,20 @@
                 re, im = triple_product(
                     load(left_ref[q]), load(middle_ref[q]), load(right_ref[q])
                 )
-                w = jnp.broadcast_to(weight_ref[pl.ds(q, 1), :], (8, half))
-                keep = jnp.broadcast_to(keep_ref[pl.ds(q, 1), :], (8, half))
+                w = jnp.broadcast_to(weight_ref[pl.ds(q, 1), :], (rows, half))
+                keep = jnp.broadcast_to(keep_ref[pl.ds(q, 1), :], (rows, half))
                 acc_re = keep * acc_re - w * im
                 acc_im = keep * acc_im + w * re
-                partial[q, 0] = acc_re
-                partial[q, 1] = acc_im
+                partial[q, 0, :rows] = acc_re
+                partial[q, 1, :rows] = acc_im
             return acc_re, acc_im
 
-        zero = jnp.zeros((8, half), jnp.float32)
+        zero = jnp.zeros((rows, half), jnp.float32)
         lax.fori_loop(0, count // unroll, chunk, (zero, zero))
 
-    def kerr(step, h, store):
-        evaluate(held[step][h])
+    def kerr(step, part, store):
+        _, source, _, _, rows = parts[step][part]
+        evaluate(source, rows)
 
         def combine(d, carry):
             for g in range(own):
@@ -425,13 +489,13 @@
                 place, has = last_ref[row], has_ref[row]
                 for r in range(2):
                     i = d * planes + 2 * g + r
-                    value = has * partial[place, r]
-                    first[i] = value
-                    mid[i] = held[step][h][i] + value
+                    value = has * partial[place, r, :rows]
+                    first[i, :rows] = value
+                    mid[i, :rows] = source[i] + value
             return carry
 
         lax.fori_loop(0, devices, combine, 0)
-        evaluate(mid)
+        evaluate(mid, rows)
 
         def finish(d, carry):
             for g in range(own):
@@ -440,15 +504,15 @@
                 squares = [0.0, 0.0]
                 for r in range(2):
                     i = d * planes + 2 * g + r
-                    second = has * partial[place, r]
-                    new = held[step][h][i] + 0.5 * (first[i] + second)
-                    estimate = 0.5 * (second - first[i])
+                    second = has * partial[place, r, :rows]
+                    new = source[i] + 0.5 * (first[i, :rows] + second)
+                    estimate = 0.5 * (second - first[i, :rows])
                     store(d, 2 * g + r, new)
                     squares[0] += estimate * estimate
                     squares[1] += new * new
                 for kind in range(2):
                     total = jnp.sum(squares[kind], axis=0, keepdims=True)
-                    if h == 0:
+                    if part == 0:
                         sums[kind, pl.ds(row, 1)] = total
                     else:
                         sums[kind, pl.ds(row, 1)] += total
@@ -461,6 +525,7 @@
             norm[pl.ds(2 * step + kind, 1)] = jnp.sum(sums[kind].T, axis=0, keepdims=True)
 
     norm[...] = jnp.zeros_like(norm)
+    loads[0].wait()
     for g in range(own):
         for t in range(tm_ways):
             octet, line = divmod(t * own + g, 8)
@@ -486,6 +551,8 @@
 
         lax.fori_loop(1, tm_ways, fetch, 0)
 
+    loads[1].wait()
+    loads[2].wait()
     for part, (m1, m2) in enumerate(((m1h, m2h), (m1l, m2l))):
         re, im = table_ref[part, 0], table_ref[part, 1]
         for table, sign in ((m1, 1), (m2, -1)):
@@ -532,11 +599,11 @@
 
         return store
 
-    arrived(held[0][0].at[pl.ds(0, (devices - 1) * planes)], 0)
+    arrived(held_00.at[pl.ds(0, (devices - 1) * planes)], 0)
     kerr(0, 0, keep_update(0))
     back[0, me] = updated[0, me]
     to_all(lambda holder: updated.at[0, holder], back.at[0, me], 2)
-    arrived(held[0][1].at[pl.ds(0, (devices - 1) * planes)], 1)
+    arrived(held_01.at[pl.ds(0, (devices - 1) * planes)], 1)
     kerr(0, 1, keep_update(1))
     back[1, me] = updated[1, me]
     for g in range(own):
@@ -550,53 +617,69 @@
 
     def load_back(g):
         arrived(back.at[1, pl.ds(0, devices - 1), pl.ds(0, 2)], 3 + g)
-        parts = []
+        pair = []
         for r in range(2):
-            parts.append(
+            pair.append(
                 jnp.concatenate(
                     [back[h, :, 2 * g + r].reshape(radix, half) for h in range(2)], axis=1
                 )
             )
-        return parts
-
-    base = 3 + own
-    spectral(load_back, 1, base)
-
-    def last_update(h):
+        return pair
+
+    spectral(load_back, 1, slot_last)
+
+    def last_update(h, row, count_rows):
         def store(d, plane, value):
             g, r = divmod(plane, 2)
             mode = d // mode_ways * own + g
-            rows = pl.ds(lax.rem(mode, 8), 8, stride=8)
+            rows = pl.ds(lax.rem(mode, 8) + 8 * row, count_rows, stride=8)
             final.reshape(2, mode_ways, 2, octets, 64, half)[
                 h, lax.rem(d, mode_ways), r, mode // 8, rows, :
             ] = value
 
         return store
 
-    def home(h, slot):
+    def home_part(i):
+        _, _, h, row, rows = parts[1][i]
+        lines = pl.ds(row, rows)
+        return (lambda mode: final.at[h, mode, :, :, lines]), out_ref.at[:, :, my_mode, lines, h]
+
+    def home_own(i):
+        source, target = home_part(i)
+        return pltpu.make_async_copy(source(my_mode), target, own_sems.at[i])
+
+    def home(i):
+        source, target = home_part(i)
+
         def one(k, carry):
             mode = lax.rem(my_mode + k, mode_ways)
             pltpu.make_async_remote_copy(
-                src_ref=final.at[h, mode],
-                dst_ref=out_ref.at[:, :, my_mode, :, h],
-                send_sem=send_sems.at[slot],
-                recv_sem=recv_sems.at[slot],
+                src_ref=source(mode),
+                dst_ref=target,
+                send_sem=send_sems.at[slot_home + i],
+                recv_sem=recv_sems.at[slot_home + i],
                 device_id=(mode, my_tm),
                 device_id_type=MESH,
             ).start()
             return carry
 
         lax.fori_loop(1, mode_ways, one, 0)
-        out_ref[:, :, my_mode, :, h] = final[h, my_mode]
-
-    for h in range(2):
-        arrived(held[1][h].at[pl.ds(0, (devices - 1) * planes)], base + h)
-        kerr(1, h, last_update(h))
-        home(h, base + 2 + h)
-    fold(1)
-    norms[me] = norm[...]
-    to_all(lambda holder: norm, norms.at[me], base + 4)
-    arrived(norms.at[pl.ds(0, devices - 1)], base + 4)
+        home_own(i).start()
+
+    def home_all(i):
+        _, _, h, row, rows = parts[1][i]
+        return final.at[h, pl.ds(0, mode_ways - 1), :, :, pl.ds(row, rows)]
+
+    for i, (_, target, h, row, rows) in enumerate(parts[1]):
+        sources = devices - 1 if i == 0 else devices - mode_ways
+        arrived(target.at[pl.ds(0, sources * planes)], slot_last + i)
+        kerr(1, i, last_update(h, row, rows))
+        if i == len(parts[1]) - 1:
+            fold(1)
+            norms[me] = norm[...]
+            to_all(lambda holder: norm, norms.at[me], slot_norm)
+        home(i)
+    arrived(norms.at[pl.ds(0, devices - 1)], slot_norm)
     total = jnp.sum(norms[...], axis=0)
     mode = lax.broadcasted_iota(jnp.int32, (devices * own, modes_local), 1)
     place = lax.broadcasted_iota(jnp.int32, (devices * own, modes_local), 0)
@@ -609,19 +692,20 @@
         ],
         axis=0,
     )
-    for h in range(2):
-        arrived(final.at[h, pl.ds(0, mode_ways - 1)], base + 2 + h)
-    for step, at in ((0, 0), (1, base)):
-        for h in range(2):
-            drained(sent.at[step, h, pl.ds(0, devices - 1)], at + h)
-    drained(updated.at[0, pl.ds(0, devices - 1)], 2)
+    for i in range(len(parts[1])):
+        arrived(home_all(i), slot_home + i)
+        drained(home_all(i), slot_home + i)
+        home_own(i).wait()
+    for step, base in ((0, 0), (1, slot_last)):
+        for i, (source, _, _, _, _) in enumerate(parts[step]):
+            sources = devices - mode_ways if step == 1 and i > 0 else devices - 1
+            drained(source.at[pl.ds(0, sources)], base + i)
+    drained(updated.at[0, pl.ds(0, devices - 1)], slot_back)
     for g in range(own):
-        drained(updated.at[1, pl.ds(0, devices - 1), pl.ds(0, 2)], 3 + g)
-    for h in range(2):
-        drained(final.at[h, pl.ds(0, mode_ways - 1)], base + 2 + h)
-    for g in range(own):
+        drained(updated.at[1, pl.ds(0, devices - 1), pl.ds(0, 2)], slot_back + 1 + g)
         drained(columns.at[g, pl.ds(0, tm_ways - 1)], head + g)
-    drained(norms.at[pl.ds(0, devices - 1)], base + 4)
+        drained(relay.at[:, :, pl.ds(0, mode_ways - 1), pl.ds(0, 2)], slot_relay + g)
+    drained(norms.at[pl.ds(0, devices - 1)], slot_norm)
 
 
 def step_all(ways, own, beta, quartets, intersections, x, table, twist):
@@ -635,22 +719,28 @@
     vmem = pl.BlockSpec(memory_space=pltpu.VMEM)
     smem = pl.BlockSpec(memory_space=pltpu.SMEM)
     real = lambda *shape: pltpu.VMEM(shape, jnp.float32)
-    slots = 8 + 2 * own
+    slots = 10 + 3 * own
+    hbm = pl.BlockSpec(memory_space=pl.ANY)
     return pl.pallas_call(
         functools.partial(step_kernel, ways, own),
-        in_specs=[smem] + [vmem] * 5,
-        out_specs=[vmem, vmem],
+        in_specs=[smem, vmem, vmem, hbm, hbm, hbm],
+        out_specs=[hbm, vmem],
         out_shape=[
             jax.ShapeDtypeStruct((2, octets, mode_ways, 8, 2, 8, half), jnp.float32),
             jax.ShapeDtypeStruct((STEPS, own * tm_ways), jnp.float32),
         ],
         scratch_shapes=[
+            real(*x.shape),
+            pltpu.VMEM(table.shape, table.dtype),
+            real(*twist.shape),
             *[pltpu.VMEM((2 * radix, 2 * radix), jnp.bfloat16)] * 4,
             real(2, own, radix, radix),
             real(own, tm_ways, 2, 2, radix // tm_ways, half),
             real(own, tm_ways, 2, 2, radix // tm_ways, half),
-            real(2, 2, devices, planes, 8, half),
-            *[real(devices * planes, 8, half)] * 4,
+            real(3, devices, planes, 8, half),
+            *[real(2, tm_ways, mode_ways, planes, 4, half)] * 2,
+            *[real(devices * planes, 8, half)] * 3,
+            *[real(devices * planes, 4, half)] * 2,
             real(devices * planes, 8, half),
             real(devices * planes, 8, half),
             real(count, 2, 8, half),
@@ -670,7 +760,8 @@
             pltpu.SMEM((half,), jnp.float32),
             pltpu.SemaphoreType.DMA((slots,)),
             pltpu.SemaphoreType.DMA((slots,)),
-            pltpu.SemaphoreType.DMA((5,)),
+            pltpu.SemaphoreType.DMA((8,)),
+            pltpu.SemaphoreType.DMA((3,)),
         ],
         compiler_params=pltpu.CompilerParams(
             vmem_limit_bytes=56 * 1024 * 1024, collective_id=0, has_side_effects=True

time: 224 us -> 214 us (0.955)
  Pallas kernels: 220 us -> 209 us
    pallas_call x1, Pallas kernels: 220 us -> 209 us  [step_all(): pl.pallas_call(functools.partial(step_kernel, ways, own), in_specs=[smem,...]
where the time goes in v3:
time: 214 us; the launch traced here: 213 us
  Pallas kernels  209 us (98%)
  local copies, waits for them, and re-layouts  3.61 us (2%)
    pallas_call x1, Pallas kernels, step_all(): pl.pallas_call(functools.partial(step_kernel, ways, own), in_specs=[smem,...  209 us

profile of v3, /device:TPU:0, one launch (start us, length us, event | category | flops | bytes accessed | tf_op | source)
XLA Modules:
  0.0 212.8 jit_solution(17626409667660875410)
XLA Ops:
  0.6 208.6 %step_all.1 = (f32[2,2,8,8,2,8,128]{6,5,4,3,2,1,0:T(8,128)}, f32[2,16]{1,0:T(2,128)}) custom-call(f32[3,16]{1,0:T(4,128)} %beta_ref.1, s32[4,1024]{1,0:T(4,128)} %quartets_ref.1, f32[1,1024]{1,0:T(1,128)} %bitcast.13, f32[2,2,1024,128]{3,2,1,0:T(8,128)} %bitcast.11, bf16[2,2,256,256]{3,2,1,0:T(8,128)(2,1)} %constant.4.clone.table_hbm, ...), custom_call_target="tpu_custom_call" | custom-call | tf_op jit(solution)/shard_map/step_all/pallas_call | solution.py:724
  209.2 0.0 copy-start
  209.2 3.0 %copy.10 = f32[2,16,16384]{2,1,0:T(8,128)} copy(f32[2,16,16384]{2,1,0:T(8,128)} %bitcast.12) | data formatting | bytes 4194304
  212.3 0.0 copy-done
  212.3 0.6 copy.11
Async XLA Ops:
  209.2 3.1 %copy-start = (f32[2,16]{1,0:T(2,128)S(1)}, f32[2,16]{1,0:T(2,128)}, u32[]{:S(2)}) copy-start(f32[2,16]{1,0:T(2,128)} %get-tuple-element.9) | copy-start | bytes 388

commit v4 on v3

--- a/solution.py
+++ b/solution.py
@@ -249,9 +249,9 @@
 
 
 def step_kernel(
-    ways, own, beta_ref, quartets_ref, intersections_ref, x_hbm, table_hbm, twist_hbm,
-    out_ref, err_ref,
-    x_ref, table_ref, twist_ref,
+    ways, own, beta_hbm, quartets_hbm, intersections_hbm, x_hbm, table_hbm, twist_hbm,
+    out_ref, err_out,
+    beta_ref, quartets_ref, intersections_ref, err_ref, x_ref, table_ref, twist_ref,
     m1h, m1l, m2h, m2l, rotor_ref, staged, columns,
     sent, short, relay, held_00, held_01, held_10, held_11, held_12, mid, first, partial, updated, back, final, sums, norm, norms,
     places, shares, spread_ref, weight_ref, keep_ref, left_ref, middle_ref, right_ref, last_ref, has_ref,
@@ -298,7 +298,14 @@
     loads = [
         pltpu.make_async_copy(src, dst, table_sems.at[5 + i])
         for i, (src, dst) in enumerate(
-            ((x_hbm, x_ref), (table_hbm, table_ref), (twist_hbm, twist_ref))
+            (
+                (x_hbm, x_ref),
+                (table_hbm, table_ref),
+                (twist_hbm, twist_ref),
+                (beta_hbm, beta_ref),
+                (quartets_hbm, quartets_ref),
+                (intersections_hbm, intersections_ref),
+            )
         )
     ]
     for copy in loads:
@@ -494,7 +501,7 @@
                     mid[i, :rows] = source[i] + value
             return carry
 
-        lax.fori_loop(0, devices, combine, 0)
+        lax.fori_loop(0, devices, combine, 0, unroll=2)
         evaluate(mid, rows)
 
         def finish(d, carry):
@@ -518,7 +525,7 @@
                         sums[kind, pl.ds(row, 1)] += total
             return carry
 
-        lax.fori_loop(0, devices, finish, 0)
+        lax.fori_loop(0, devices, finish, 0, unroll=2)
 
     def fold(step):
         for kind in range(2):
@@ -551,8 +558,8 @@
 
         lax.fori_loop(1, tm_ways, fetch, 0)
 
-    loads[1].wait()
-    loads[2].wait()
+    for copy in loads[1:]:
+        copy.wait()
     for part, (m1, m2) in enumerate(((m1h, m2h), (m1l, m2l))):
         re, im = table_ref[part, 0], table_ref[part, 1]
         for table, sign in ((m1, 1), (m2, -1)):
@@ -692,6 +699,8 @@
         ],
         axis=0,
     )
+    err_copy = pltpu.make_async_copy(err_ref, err_out, table_sems.at[11])
+    err_copy.start()
     for i in range(len(parts[1])):
         arrived(home_all(i), slot_home + i)
         drained(home_all(i), slot_home + i)
@@ -706,6 +715,7 @@
         drained(columns.at[g, pl.ds(0, tm_ways - 1)], head + g)
         drained(relay.at[:, :, pl.ds(0, mode_ways - 1), pl.ds(0, 2)], slot_relay + g)
     drained(norms.at[pl.ds(0, devices - 1)], slot_norm)
+    err_copy.wait()
 
 
 def step_all(ways, own, beta, quartets, intersections, x, table, twist):
@@ -716,20 +726,22 @@
     radix = twist.shape[1]
     half = radix // 2
     octets = x.shape[1]
-    vmem = pl.BlockSpec(memory_space=pltpu.VMEM)
-    smem = pl.BlockSpec(memory_space=pltpu.SMEM)
     real = lambda *shape: pltpu.VMEM(shape, jnp.float32)
     slots = 10 + 3 * own
     hbm = pl.BlockSpec(memory_space=pl.ANY)
     return pl.pallas_call(
         functools.partial(step_kernel, ways, own),
-        in_specs=[smem, vmem, vmem, hbm, hbm, hbm],
-        out_specs=[hbm, vmem],
+        in_specs=[hbm] * 6,
+        out_specs=[pl.BlockSpec(memory_space=pltpu.VMEM)] * 2,
         out_shape=[
-            jax.ShapeDtypeStruct((2, octets, mode_ways, 8, 2, 8, half), jnp.float32),
-            jax.ShapeDtypeStruct((STEPS, own * tm_ways), jnp.float32),
+            pltpu.VMEM((2, octets, mode_ways, 8, 2, 8, half), jnp.float32),
+            pltpu.VMEM((STEPS, own * tm_ways), jnp.float32),
         ],
         scratch_shapes=[
+            pltpu.SMEM(beta.shape, beta.dtype),
+            pltpu.VMEM(quartets.shape, quartets.dtype),
+            real(1, count),
+            real(STEPS, own * tm_ways),
             real(*x.shape),
             pltpu.VMEM(table.shape, table.dtype),
             real(*twist.shape),
@@ -760,14 +772,37 @@
             pltpu.SMEM((half,), jnp.float32),
             pltpu.SemaphoreType.DMA((slots,)),
             pltpu.SemaphoreType.DMA((slots,)),
-            pltpu.SemaphoreType.DMA((8,)),
+            pltpu.SemaphoreType.DMA((12,)),
             pltpu.SemaphoreType.DMA((3,)),
         ],
         compiler_params=pltpu.CompilerParams(
-            vmem_limit_bytes=56 * 1024 * 1024, collective_id=0, has_side_effects=True
+            vmem_limit_bytes=52 * 1024 * 1024, collective_id=0, has_side_effects=True
         ),
         name="step_all",
     )(beta, quartets, intersections[None], x, table, twist)
+
+
+def emit_kernel(out_ref, err_ref, out_hbm, err_hbm, sems):
+    copies = [
+        pltpu.make_async_copy(out_ref, out_hbm, sems.at[0]),
+        pltpu.make_async_copy(err_ref, err_hbm, sems.at[1]),
+    ]
+    for copy in copies:
+        copy.start()
+    for copy in copies:
+        copy.wait()
+
+
+def emit(out, errors):
+    return pl.pallas_call(
+        emit_kernel,
+        in_specs=[pl.BlockSpec(memory_space=pltpu.VMEM)] * 2,
+        out_specs=[pl.BlockSpec(memory_space=pl.ANY)] * 2,
+        out_shape=[jax.ShapeDtypeStruct(a.shape, jnp.float32) for a in (out, errors)],
+        scratch_shapes=[pltpu.SemaphoreType.DMA((2,))],
+        compiler_params=pltpu.CompilerParams(vmem_limit_bytes=1024 * 1024),
+        name="emit",
+    )(out, errors)
 
 
 def constant_tables(radix):
@@ -791,7 +826,7 @@
     octets, tiles = modes_local // 8, time_local // 128
     x = field.reshape(2, octets, 8, tiles, 128).transpose(0, 1, 3, 2, 4)
     x = x.reshape(2, octets, tiles * 8, 128)
-    out, errors = step_all(ways, own, beta, quartets, intersections, x, table, twist)
+    out, errors = emit(*step_all(ways, own, beta, quartets, intersections, x, table, twist))
     out = out.reshape(2, octets, tiles, 8, 128).transpose(0, 1, 3, 2, 4)
     return (out.reshape(2, modes_local, time_local), errors)
 

time: 214 us -> 209 us (0.977)
  local copies, waits for them, and re-layouts: 3.61 us -> 0 us
    unnamed x4 -> x0, local copies, waits for them, and re-layouts: 3.61 us -> none
    pallas_call x1 -> x2, Pallas kernels: 209 us -> 208 us  [the longest x1 207 us: step_all(): pl.pallas_call(functools.partial(step_kernel, ways, own), in_specs=[hbm]...]
where the time goes in v4:
time: 209 us
  Pallas kernels  208 us (100%)
    pallas_call x1, Pallas kernels, step_all(): pl.pallas_call(functools.partial(step_kernel, ways, own), in_specs=[hbm]...  207 us

profile of v4, /device:TPU:0, one launch (start us, length us, event | category | flops | bytes accessed | tf_op | source)
XLA Modules:
  0.0 208.6 jit_solution(7375513392669128828)
XLA Ops:
  0.6 206.7 %step_all.1 = (f32[2,2,8,8,2,8,128]{6,5,4,3,2,1,0:T(8,128)S(1)}, f32[2,16]{1,0:T(2,128)S(1)}) custom-call(f32[3,16]{1,0:T(4,128)} %beta_hbm.1, s32[4,1024]{1,0:T(4,128)} %quartets_hbm.1, f32[1,1024]{1,0:T(1,128)} %bitcast.12, f32[2,2,1024,128]{3,2,1,0:T(8,128)} %bitcast.11, bf16[2,2,256,256]{3,2,1,0:T(8,128)(2,1)} %constant.4.clone.table_hbm, ...), custom_call_target="tpu_custom_call" | custom-call | tf_op jit(solution)/shard_map/step_all/pallas_call | solution.py:732
  207.3 1.3 emit.1
